TPU v7x, 32 devices: a whole 2x2x4 slice. The times are simulated.
32 devices in a mesh: gx: 8 (over z, y), gy: 4 (over x, core).
Axes of the slice: x: 2, y: 2, z: 4, core: 2. Of those that a mesh axis runs over, the one named last changes fastest.
Arguments:
- populations: float32 [27, 16, 32, 128], P(None, 'gx', 'gy'), as said below
- relax: float32 [27], replicated, may hold values from 0.6 to 1.9
- solid: int32 [16, 32, 128], P('gx', 'gy'), may hold values 0 or 1
- wall_cell: int32 [8, 4, 256], P('gx', 'gy'), may hold values from 0 to 2047, as said below
- wall_normal: int32 [8, 4, 256], P('gx', 'gy'), may hold values from 0 to 5
- wall_count: int32 [8, 4], P('gx', 'gy'), may hold values from 1 to 256, as said below
- sample_ref: int32 [8, 4, 256], P('gx', 'gy'), may hold values from 0 to 255, each once within a row
- stencil_cell: int32 [8, 4, 8, 256], P('gx', 'gy'), may hold values from 0 to 2047, as said below
- stencil_weight: float32 [8, 4, 8, 256], P('gx', 'gy'), may hold values from 0 to 1, as said below
Outputs:
- read: float32 [27, 16, 32, 128], P(None, 'gx', 'gy')
Inputs may be any that keep to these rules, and one draw needn't show every extreme that they name: `populations`: positive everywhere. `wall_cell`: the 256 entries of one device are distinct local cells. Slots 0 to wall_count - 1 of a device are live; some device has all 256 live. `stencil_cell`: the eight corners of a unit cube of the owner's local cells, wrapping along z only. `stencil_weight`: nonnegative trilinear weights, summing to one over the eight corners.
All inputs are finite; a program needn't handle non-finite values. No bound on the sum of `solid` on one device may be relied on, other than what follows from the above.
Results may differ from a plain program's by a relative error of at most 0.0003.
Values sent between devices are 32-bit elements; how exact they have to be, the bound alone decides.
A program may use at most 64 MiB of HBM per device.

v0:
```python
import functools

import jax
import jax.numpy as jnp
import numpy as np
from jax import lax
from jax.experimental import pallas as pl
from jax.experimental.pallas import tpu as pltpu
from jax.sharding import PartitionSpec as P

steps = np.array([(a - 1, b - 1, c - 1) for a in range(3) for b in range(3) for c in range(3)])
wall_ratio = (1.0 / 9.0) ** (1.0 / 7.0)
weights = np.prod(np.where(steps == 0, 2.0 / 3.0, 1.0 / 6.0), axis=1)
vander = np.array([[1.0, 1.0, 1.0], [-1.0, 0.0, 1.0], [1.0, 0.0, 1.0]])
moment = np.kron(np.kron(vander, vander), vander)
LANES = 128
MESH = pl.DeviceIdType.MESH


def equilibrium_moments():
    x, y, z = steps.T.astype(float)
    basis = np.stack(
        [
            np.ones(27),
            3 * x,
            3 * y,
            3 * z,
            4.5 * x * x - 1.5,
            4.5 * y * y - 1.5,
            4.5 * z * z - 1.5,
            9 * x * y,
            9 * x * z,
            9 * y * z,
        ],
        axis=1,
    )
    return moment @ (weights[:, None] * basis)


def forward(vals):
    for stride in (9, 3, 1):
        out = list(vals)
        for i in range(27):
            if i // stride % 3 == 0:
                lo, mid, hi = (vals[i], vals[i + stride], vals[i + 2 * stride])
                both = lo + hi
                out[i], out[i + stride], out[i + 2 * stride] = (both + mid, hi - lo, both)
        vals = out
    return vals


def plus(a, b):
    return b if a is None else a if b is None else a + b


def minus(a, b):
    return a if b is None else -b if a is None else a - b


def backward(vals):
    for stride in (9, 3, 1):
        out = list(vals)
        for i in range(27):
            if i // stride % 3 == 0:
                s0, s1, s2 = (vals[i], vals[i + stride], vals[i + 2 * stride])
                out[i], out[i + stride], out[i + 2 * stride] = (
                    minus(s2, s1),
                    minus(s0, s2),
                    plus(s2, s1),
                )
        vals = out
    return vals


def combine(terms):
    total = None
    for factor, value in terms:
        if abs(factor) < 1e-12:
            continue
        if abs(factor - 1.0) < 1e-12:
            total = plus(total, value)
        elif abs(factor + 1.0) < 1e-12:
            total = minus(total, value)
        else:
            total = plus(total, value * np.float32(factor))
    return total


def roll(value, shift, axis):
    return value if shift == 0 else pltpu.roll(value, shift % value.shape[axis], axis)


def lane_gather(row, index):
    return jnp.take_along_axis(
        jnp.broadcast_to(row, index.shape), index, axis=1, mode="promise_in_bounds"
    )


def kernel(
    devices_x,
    devices_y,
    pop_hbm,
    relax,
    solid_hbm,
    wall_hbm,
    normal_hbm,
    count,
    ref_hbm,
    stencil_hbm,
    weight_hbm,
    out,
    pop,
    solid,
    wall,
    normal,
    ref,
    stencil,
    weight,
    vel,
    samples,
    rx,
    post,
    settled,
    fields,
    shifted,
    stage_y,
    stage_c,
    stage_s,
    stage_f,
    stage_d,
    got_x,
    got_y,
    got_c,
    got_sx,
    got_sy,
    got_fx,
    got_fy,
    got_fc,
    lines,
    line_fields,
    masks,
    load_sem,
    send_sem,
    recv_sem,
):
    size_x, size_y = pop.shape[1:3]
    rows = size_x * size_y
    slots_all = wall.shape[2]
    slots = slots_all // devices_y
    shift_bits = slots.bit_length() - 1
    my_x = lax.axis_index("gx")
    my_y = lax.axis_index("gy")

    def at(dx, dy):
        return {
            "gx": lax.rem(my_x + (dx + devices_x), devices_x),
            "gy": lax.rem(my_y + (dy + devices_y), devices_y),
        }

    loads = [
        pltpu.make_async_copy(src, dst, load_sem.at[n])
        for n, (src, dst) in enumerate(
            [
                (pop_hbm, pop),
                (stencil_hbm, stencil),
                (weight_hbm, weight),
                (solid_hbm, solid),
                (wall_hbm, wall),
                (normal_hbm, normal),
                (ref_hbm, ref),
            ]
        )
    ]
    for load in loads:
        load.start()
    greeted = [(dx, dy) for dx in (-1, 0, 1) for dy in range(devices_y) if (dx, dy) != (0, 0)]
    barrier = pltpu.get_barrier_semaphore()
    for dx, dy in greeted:
        pl.semaphore_signal(barrier, inc=1, device_id=at(dx, dy), device_id_type=MESH)

    sent = []

    def send(src, dst, dx, dy):
        n = len(sent)
        copy = pltpu.make_async_remote_copy(
            src_ref=src,
            dst_ref=dst,
            send_sem=send_sem.at[n],
            recv_sem=recv_sem.at[n],
            device_id=at(dx, dy),
            device_id_type=MESH,
        )
        copy.start()
        sent.append(copy)
        return copy

    loads[0].wait()
    moments, speeds = ([], [])
    for x in range(size_x):
        found = forward([pop[i, x] * np.float32(weights[i]) for i in range(27)])
        rho = found[0]
        inverse = 1.0 / rho
        u = [found[9] * inverse, found[3] * inverse, found[1] * inverse]
        for c in range(3):
            vel[c * rows + x * size_y : c * rows + (x + 1) * size_y, :] = u[c]
        for f, value in enumerate([rho] + u):
            fields[f, x] = value
        moments.append(found)
        speeds.append(u)

    loads[1].wait()
    loads[2].wait()
    for tile in range(slots_all // LANES):
        lanes = slice(tile * LANES, (tile + 1) * LANES)
        cell = stencil[0, 0, :, lanes]
        lane = jnp.bitwise_and(cell, LANES - 1)
        row = jnp.right_shift(cell, 7)
        picked = [jnp.zeros(cell.shape, jnp.float32)] * 3
        for r in range(rows):
            here = row == r
            for c in range(3):
                picked[c] = jnp.where(
                    here, lane_gather(vel[c * rows + r : c * rows + r + 1, :], lane), picked[c]
                )
        factor = weight[0, 0, :, lanes]
        for c in range(3):
            n = tile * 3 + c
            samples[n : n + 1, :] = jnp.sum(picked[c] * factor, axis=0, keepdims=True)
    rx[1, my_y] = samples[...]

    loads[3].wait()
    for side, y in ((0, size_y - 1), (1, 0)):
        for x in range(size_x):
            stage_s[side, x : x + 1, :] = solid[x, y : y + 1, :]

    coefficient = equilibrium_moments()
    for x in range(size_x):
        found, (ux, uy, uz) = (moments[x], speeds[x])
        rho, mx, my, mz = (found[0], found[9], found[3], found[1])
        basis = [rho, mx, my, mz, mx * ux, my * uy, mz * uz, mx * uy, mx * uz, my * uz]
        deviation = []
        for j in range(27):
            if j in (0, 1, 3, 9):
                deviation.append(None)
            else:
                balance = combine(list(zip(coefficient[j], basis)))
                deviation.append(minus(found[j], balance) * relax[j])
        change = backward(deviation)
        for i in range(27):
            half = 0.5 ** int(np.sum(steps[i] != 0)) / weights[i]
            post[i, x] = pop[i, x] - change[i] * np.float32(half)

    for load in loads[4:]:
        load.wait()
    cell = wall[0]
    slot = lax.broadcasted_iota(jnp.int32, (1, slots_all), 1)
    live = slot < count[0, 0]
    which = ref[0]
    offset = lax.rem(my_y * slots, LANES)
    row_hit = jnp.logical_and(
        lax.broadcasted_iota(jnp.int32, (rows, slots_all), 0) == jnp.right_shift(cell, 7), live
    )
    values = [
        jnp.right_shift(which, shift_bits) + 1,
        jnp.bitwise_and(which, slots - 1) + offset,
        jnp.right_shift(normal[0], 1),
    ]
    left = jnp.concatenate(
        [jnp.where(row_hit, value.astype(jnp.float32), 0.0) for value in values], axis=0
    ).astype(jnp.bfloat16)
    right = jnp.where(
        lax.broadcasted_iota(jnp.int32, (LANES, slots_all), 0)
        == jnp.bitwise_and(cell, LANES - 1),
        1.0,
        0.0,
    ).astype(jnp.bfloat16)
    table = lax.dot_general(
        left, right, (((1,), (1,)), ((), ())), preferred_element_type=jnp.float32
    )
    for n in range(3):
        for x in range(size_x):
            first = n * rows + x * size_y
            fields[4 + n, x] = table[first : first + size_y]

    for i in range(27):
        a, b, c = steps[i]
        if b == 0:
            continue
        side = 0 if b > 0 else 1
        edge = size_y - 1 if b > 0 else 0
        for x in range(size_x):
            line = post[i, x, edge : edge + 1, :]
            if 0 <= x + a < size_x:
                n = ((a + 1) * 3 + c + 1) * size_x + x
                stage_y[side, n : n + 1, :] = line
            else:
                stage_c[0 if a > 0 else 1, side, c + 1 : c + 2, :] = line
    for side, y in ((0, size_y - 1), (1, 0)):
        for f in range(7):
            for x in range(size_x):
                n = f * size_x + x
                stage_f[side, n : n + 1, :] = fields[f, x, y : y + 1, :]
            for way, x in ((0, size_x - 1), (1, 0)):
                stage_d[way, side, f : f + 1, :] = fields[f, x, y : y + 1, :]
        for way, x in ((0, size_x - 1), (1, 0)):
            stage_d[way, side, 7:8, :] = solid[x, y : y + 1, :].astype(jnp.float32)
    pl.semaphore_wait(barrier, len(greeted))
    sample_copies = [send(samples, rx.at[1 - dx, my_y], dx, dy) for dx, dy in greeted]
    solid_copies = [
        send(solid.at[size_x - 1], got_sx.at[0], 1, 0),
        send(solid.at[0], got_sx.at[1], -1, 0),
    ]
    for side, dy in ((0, 1), (1, -1)):
        solid_copies.append(send(stage_s.at[side], got_sy.at[side], 0, dy))
    early = [
        send(post.at[18:27, size_x - 1], got_x.at[0], 1, 0),
        send(post.at[0:9, 0], got_x.at[1], -1, 0),
        send(fields.at[:, size_x - 1], got_fx.at[0], 1, 0),
        send(fields.at[:, 0], got_fx.at[1], -1, 0),
    ]
    for side, dy in ((0, 1), (1, -1)):
        for way, dx in ((0, 1), (1, -1)):
            early.append(send(stage_c.at[way, side], got_c.at[way, side], dx, dy))
            early.append(send(stage_d.at[way, side], got_fc.at[way, side], dx, dy))
        early.append(send(stage_y.at[side], got_y.at[side], 0, dy))
        early.append(send(stage_f.at[side], got_fy.at[side], 0, dy))

    for copy in sample_copies:
        copy.wait_recv()

    def velocity(field, owner, groups):
        source, lane, axis = [value.astype(jnp.int32) for value in field[4:]]
        lane = jnp.bitwise_and(lane, LANES - 1)
        tile = (owner * slots) // LANES
        new = []
        for c in range(3):
            value = jnp.zeros((size_y, LANES), jnp.float32)
            for group, mask in groups:
                for peer in range(devices_y):
                    here = source == peer + 1
                    if mask is not None:
                        here = jnp.logical_and(here, mask)
                    line = rx[group, peer, pl.ds(tile * 3 + c, 1), :]
                    value = jnp.where(here, lane_gather(line, lane), value)
            value = jnp.where(axis == c, 0.0, value * np.float32(wall_ratio))
            new.append(jnp.where(source > 0, value, field[1 + c]))
        return new

    def correction(rho, u, new, wanted):
        linear = [3.0 * rho * (new[c] - u[c]) for c in range(3)]
        pure = [rho * (new[c] * new[c] - u[c] * u[c]) for c in range(3)]
        rest = -1.5 * (pure[0] + pure[1] + pure[2])
        pure = [4.5 * value for value in pure]
        mixed = {
            (c, d): 9.0 * rho * (new[c] * new[d] - u[c] * u[d])
            for c, d in ((0, 1), (0, 2), (1, 2))
        }
        halves, found = ({}, {})
        for i in wanted:
            first = min(i, 26 - i)
            if first not in halves:
                step = steps[first]
                even, odd = (rest, None)
                for c in range(3):
                    if step[c] != 0:
                        even = even + pure[c]
                        odd = plus(odd, linear[c]) if step[c] > 0 else minus(odd, linear[c])
                for c, d in mixed:
                    if step[c] * step[d] > 0:
                        even = even + mixed[c, d]
                    elif step[c] * step[d] < 0:
                        even = even - mixed[c, d]
                halves[first] = (even, odd)
            even, odd = halves[first]
            found[i] = even if odd is None else even + odd if i == first else even - odd
        return found

    for x in range(size_x):
        field = [fields[f, x] for f in range(7)]
        found = correction(field[0], field[1:4], velocity(field, my_y, [(1, None)]), range(27))
        for i in range(27):
            a, b, c = steps[i]
            value = post[i, x] + found[i]
            settled[i, x] = value
            shifted[i, x] = roll(roll(value, b, 0), c, 1)

    for copy in solid_copies:
        copy.wait_recv()
    line_of = lax.broadcasted_iota(jnp.int32, (size_y, LANES), 0)

    def mend(value, line, b):
        edge = 0 if b > 0 else size_y - 1
        return jnp.where(line_of == edge, jnp.broadcast_to(line, value.shape), value)

    def mark(x):
        plane = got_sx[0] if x < 0 else got_sx[1] if x == size_x else solid[x]
        for b in (-1, 0, 1):
            value = roll(plane, b, 0)
            if b != 0:
                side = 0 if b > 0 else 1
                if x < 0:
                    line = got_fc[0, side, 7:8, :].astype(jnp.int32)
                elif x == size_x:
                    line = got_fc[1, side, 7:8, :].astype(jnp.int32)
                else:
                    line = got_sy[side, x : x + 1, :]
                value = mend(value, line, b)
            for c in (-1, 0, 1):
                masks[(b + 1) * 3 + c + 1, x + 1] = roll(value, c, 1)

    for x in range(size_x):
        mark(x)

    def gather_rows(target, index, straight, corner, f):
        for x in range(size_x):
            n = f * size_x + x
            target[index + (slice(x, x + 1),)] = straight[n : n + 1, :]
        target[index + (slice(size_x, size_x + 1),)] = corner[0][f : f + 1, :]
        target[index + (slice(size_x + 1, size_x + 2),)] = corner[1][f : f + 1, :]

    for copy in early:
        copy.wait_recv()
    mark(-1)
    mark(size_x)
    for side in range(2):
        for j in range(9):
            a, c = (j // 3 - 1, j % 3 - 1)
            for x in range(size_x):
                if 0 <= x + a < size_x:
                    n = j * size_x + x
                    lines[side, j, x : x + 1, :] = got_y[side, n : n + 1, :]
            if a != 0:
                way = 0 if a > 0 else 1
                lines[side, j, size_x + way : size_x + way + 1, :] = got_c[
                    way, side, c + 1 : c + 2, :
                ]
        for f in range(7):
            gather_rows(
                line_fields, (side, f), got_fy.at[side], [got_fc.at[way, side] for way in (0, 1)], f
            )

    border = {}
    for side, b in ((0, 1), (1, -1)):
        wanted = [i for i in range(27) if steps[i][1] == b]
        field = [line_fields[side, f] for f in range(7)]
        owner = lax.rem(my_y + (devices_y - b), devices_y)
        groups = [(1, line_of < size_x), (0, line_of == size_x), (2, line_of == size_x + 1)]
        found = correction(field[0], field[1:4], velocity(field, owner, groups), wanted)
        for i in wanted:
            a, _, c = steps[i]
            border[i] = roll(lines[side, (a + 1) * 3 + c + 1] + found[i], c, 1)
    planes = {}
    for way, a in ((0, 1), (1, -1)):
        wanted = [i for i in range(27) if steps[i][0] == a]
        field = [got_fx[way, f] for f in range(7)]
        found = correction(
            field[0], field[1:4], velocity(field, my_y, [(0 if a > 0 else 2, None)]), wanted
        )
        for i in wanted:
            _, b, c = steps[i]
            planes[i] = roll(roll(got_x[way, i % 9] + found[i], b, 0), c, 1)
    for i in range(27):
        a, b, c = steps[i]
        for x in range(size_x):
            origin = x - a
            inside = 0 <= origin < size_x
            value = shifted[i, origin] if inside else planes[i]
            if b != 0:
                n = origin if inside else size_x + (0 if a > 0 else 1)
                value = mend(value, border[i][n : n + 1, :], b)
            blocked = masks[(b + 1) * 3 + c + 1, origin + 1] != 0
            out[i, x] = jnp.where(blocked, settled[26 - i, x], value)
    for copy in sent:
        copy.wait_send()


def write_out(source, out, sem):
    copy = pltpu.make_async_copy(source, out, sem)
    copy.start()
    copy.wait()


def local(populations, relax, solid, wall_cell, wall_normal, wall_count, sample_ref, cells, factors):
    devices_x, devices_y = (lax.axis_size("gx"), lax.axis_size("gy"))
    size_x, size_y, size_z = populations.shape[1:]
    slots_all = wall_cell.shape[2]
    slots = slots_all // devices_y
    assert size_z == LANES and LANES % slots == 0 and slots & (slots - 1) == 0
    assert slots_all % LANES == 0 and devices_x > 2 and devices_y > 2
    f32, i32 = (jnp.float32, jnp.int32)
    lines = -(-9 * size_x // 8) * 8
    assert size_x + 2 <= size_y == 8
    few = -(-7 * size_x // 8) * 8
    held = -(-3 * slots_all // LANES // 8) * 8
    sends = 3 * devices_y - 1 + 4 + 16
    vmem = pltpu.VMEM
    tile = (size_y, LANES)
    anywhere = pl.BlockSpec(memory_space=pl.ANY)
    smem = pl.BlockSpec(memory_space=pltpu.SMEM)
    result = pl.pallas_call(
        functools.partial(kernel, devices_x, devices_y),
        out_shape=pltpu.VMEM(populations.shape, f32),
        in_specs=[
            anywhere,
            smem,
            anywhere,
            anywhere,
            anywhere,
            smem,
            anywhere,
            anywhere,
            anywhere,
        ],
        out_specs=pl.BlockSpec(memory_space=pltpu.VMEM),
        scratch_shapes=[
            vmem(populations.shape, f32),
            vmem(solid.shape, i32),
            vmem(wall_cell.shape, i32),
            vmem(wall_normal.shape, i32),
            vmem(sample_ref.shape, i32),
            vmem(cells.shape, i32),
            vmem(factors.shape, f32),
            vmem((3 * size_x * size_y, LANES), f32),
            vmem((held, LANES), f32),
            vmem((3, devices_y, held, LANES), f32),
            vmem(populations.shape, f32),
            vmem(populations.shape, f32),
            vmem((7, size_x) + tile, f32),
            vmem(populations.shape, f32),
            vmem((2, lines, LANES), f32),
            vmem((2, 2, 8, LANES), f32),
            vmem((2, 8, LANES), i32),
            vmem((2, few, LANES), f32),
            vmem((2, 2, 8, LANES), f32),
            vmem((2, 9) + tile, f32),
            vmem((2, lines, LANES), f32),
            vmem((2, 2, 8, LANES), f32),
            vmem((2,) + tile, i32),
            vmem((2, 8, LANES), i32),
            vmem((2, 7) + tile, f32),
            vmem((2, few, LANES), f32),
            vmem((2, 2, 8, LANES), f32),
            vmem((2, 9, 8, LANES), f32),
            vmem((2, 7, 8, LANES), f32),
            vmem((9, size_x + 2) + tile, i32),
            pltpu.SemaphoreType.DMA((7,)),
            pltpu.SemaphoreType.DMA((sends,)),
            pltpu.SemaphoreType.DMA((sends,)),
        ],
        compiler_params=pltpu.CompilerParams(collective_id=0, has_side_effects=True),
        name="lattice_step",
    )(populations, relax, solid, wall_cell, wall_normal, wall_count, sample_ref, cells, factors)
    result = pltpu.with_memory_space_constraint(result, pltpu.VMEM)
    return pl.pallas_call(
        write_out,
        out_shape=jax.ShapeDtypeStruct(populations.shape, f32),
        in_specs=[pl.BlockSpec(memory_space=pltpu.VMEM)],
        out_specs=anywhere,
        scratch_shapes=[pltpu.SemaphoreType.DMA],
        name="write_out",
    )(result)


def solution(mesh):
    return jax.shard_map(
        local,
        mesh=mesh,
        in_specs=(
            P(None, "gx", "gy", None),
            P(),
            P("gx", "gy", None),
            P("gx", "gy", None),
            P("gx", "gy", None),
            P("gx", "gy"),
            P("gx", "gy", None),
            P("gx", "gy", None, None),
            P("gx", "gy", None, None),
        ),
        out_specs=P(None, "gx", "gy", None),
        check_vma=False,
    )
```

profile of v0, /device:TPU:0, one launch (start us, length us, event | category | flops | bytes accessed | tf_op | source)
XLA Modules:
  0.0 13.8 jit_solution(6039932133528477147)
XLA Ops:
  0.7 12.4 %lattice_step.1.source = f32[27,2,8,128]{3,2,1,0:T(8,128)S(1)} custom-call(f32[27,2,8,128]{3,2,1,0:T(8,128)} %pop_hbm.1, f32[27]{0:T(128)} %relax.1, s32[2,8,128]{2,1,0:T(8,128)} %solid_hbm.1, s32[1,1,256]{2,1,0:T(1,128)} %wall_hbm.1, s32[1,1,256]{2,1,0:T(1,128)} %normal_hbm.1, s32[1,1]{1,0:T(1,128)S(6)} %copy.10.count, s32[1,1,256]{2,1,0:T(1,128)} %ref_hbm.1, ...), custom_call_target="tpu_custom_call" | custom-call | tf_op jit(solution)/shard_map/lattice_step/pallas_call | solution.py:500
  13.1 0.7 %write_out.1 = f32[27,2,8,128]{3,2,1,0:T(8,128)} custom-call(f32[27,2,8,128]{3,2,1,0:T(8,128)S(1)} %lattice_step.1.source), custom_call_target="tpu_custom_call" | custom-call | tf_op jit(solution)/shard_map/write_out/pallas_call | solution.py:554
where the time goes:
time: 13.9 us; the launch traced here: 13.8 us
  Pallas kernels  13.1 us (94%)
  between operations  0.66 us (5%)
    pallas_call x1, Pallas kernels, local(): pl.pallas_call(functools.partial(kernel, devices_x, devices_y), out_shape...  12.4 us
    pallas_call x1, Pallas kernels, local(): pl.pallas_call(write_out, out_shape=jax.ShapeDtypeStruct(populations.shap...  0.7 us

commit v1 on v0

v1 whole, which is shorter than its diff:
```python
import functools

import jax
import jax.numpy as jnp
import numpy as np
from jax import lax
from jax.experimental import pallas as pl
from jax.experimental.pallas import tpu as pltpu
from jax.sharding import PartitionSpec as P

steps = np.array([(a - 1, b - 1, c - 1) for a in range(3) for b in range(3) for c in range(3)])
wall_ratio = (1.0 / 9.0) ** (1.0 / 7.0)
weights = np.prod(np.where(steps == 0, 2.0 / 3.0, 1.0 / 6.0), axis=1)
vander = np.array([[1.0, 1.0, 1.0], [-1.0, 0.0, 1.0], [1.0, 0.0, 1.0]])
moment = np.kron(np.kron(vander, vander), vander)
LANES = 128
MESH = pl.DeviceIdType.MESH


def equilibrium_moments():
    x, y, z = steps.T.astype(float)
    basis = np.stack(
        [
            np.ones(27),
            3 * x,
            3 * y,
            3 * z,
            4.5 * x * x - 1.5,
            4.5 * y * y - 1.5,
            4.5 * z * z - 1.5,
            9 * x * y,
            9 * x * z,
            9 * y * z,
        ],
        axis=1,
    )
    return moment @ (weights[:, None] * basis)


def forward(vals):
    for stride in (9, 3, 1):
        out = list(vals)
        for i in range(27):
            if i // stride % 3 == 0:
                lo, mid, hi = (vals[i], vals[i + stride], vals[i + 2 * stride])
                both = lo + hi
                out[i], out[i + stride], out[i + 2 * stride] = (both + mid, hi - lo, both)
        vals = out
    return vals


def plus(a, b):
    return b if a is None else a if b is None else a + b


def minus(a, b):
    return a if b is None else -b if a is None else a - b


def backward(vals):
    for stride in (9, 3, 1):
        out = list(vals)
        for i in range(27):
            if i // stride % 3 == 0:
                s0, s1, s2 = (vals[i], vals[i + stride], vals[i + 2 * stride])
                out[i], out[i + stride], out[i + 2 * stride] = (
                    minus(s2, s1),
                    minus(s0, s2),
                    plus(s2, s1),
                )
        vals = out
    return vals


def combine(terms):
    total = None
    for factor, value in terms:
        if abs(factor) < 1e-12:
            continue
        if abs(factor - 1.0) < 1e-12:
            total = plus(total, value)
        elif abs(factor + 1.0) < 1e-12:
            total = minus(total, value)
        else:
            total = plus(total, value * np.float32(factor))
    return total


def roll(value, shift, axis):
    return value if shift == 0 else pltpu.roll(value, shift % value.shape[axis], axis)


def lane_gather(row, index):
    return jnp.take_along_axis(
        jnp.broadcast_to(row, index.shape), index, axis=1, mode="promise_in_bounds"
    )


def kernel(
    devices_x,
    devices_y,
    pop_hbm,
    relax_hbm,
    solid_hbm,
    wall_hbm,
    normal_hbm,
    count_hbm,
    ref_hbm,
    stencil_hbm,
    weight_hbm,
    out,
    pop,
    relax,
    count,
    solid,
    lists,
    stencil,
    weight,
    vel,
    samples,
    rx_row,
    rx_x,
    post,
    settled,
    shifted,
    fields,
    face,
    near,
    corner,
    got_face,
    got_near,
    got_corner,
    lines,
    masks,
    moved,
    tally,
    load_sem,
    send_sem,
    near_sem,
    face_sem,
    far_sem,
):
    size_x, size_y = pop.shape[1:3]
    rows = size_x * size_y
    slots_all = lists.shape[2]
    slots = slots_all // devices_y
    shift_bits = slots.bit_length() - 1
    my_x = lax.axis_index("gx")
    my_y = lax.axis_index("gy")
    ratio = np.float32(wall_ratio)
    tile = (size_y, LANES)

    def wrap(value, size):
        return jnp.where(value < 0, value + size, jnp.where(value >= size, value - size, value))

    loads = [
        pltpu.make_async_copy(src, dst, load_sem.at[n])
        for n, src, dst in [
            (0, pop_hbm, pop),
            (1, stencil_hbm, stencil),
            (2, weight_hbm, weight),
            (3, wall_hbm.at[0], lists.at[0]),
            (3, normal_hbm.at[0], lists.at[1]),
            (3, ref_hbm.at[0], lists.at[2]),
            (4, count_hbm, count),
            (5, solid_hbm, solid),
            (6, relax_hbm, relax),
        ]
    ]
    for load in loads:
        load.start()
    barrier = pltpu.get_barrier_semaphore()
    columns = {dy: wrap(my_y + dy, devices_y) for dy in range(devices_y)}
    columns[-1] = columns[devices_y - 1]
    beside = {dx: wrap(my_x + dx, devices_x) for dx in (-1, 0, 1)}
    peers = [(dx, dy) for dx in (-1, 1, 0) for dy in range(devices_y) if (dx, dy) != (0, 0)]
    for dx, dy in peers:
        pl.semaphore_signal(
            barrier,
            inc=1,
            device_id={"gx": beside[dx], "gy": columns[dy]},
            device_id_type=MESH,
        )
    for n in (0, 1, 2):
        loads[n].wait()
    pltpu.make_async_copy(lists, lists, load_sem.at[3]).wait()
    for n in (6, 7, 8):
        loads[n].wait()

    row_line = lax.broadcasted_iota(jnp.int32, tile, 0)

    moments, speeds = ([], [])
    for x in range(size_x):
        found = forward([pop[i, x] * np.float32(weights[i]) for i in range(27)])
        rho = found[0]
        inverse = 1.0 / rho
        u = [found[9] * inverse, found[3] * inverse, found[1] * inverse]
        for c in range(3):
            vel[c * rows + x * size_y : c * rows + (x + 1) * size_y, :] = u[c]
        moments.append(found)
        speeds.append(u)

    cell = lists[0]
    slot = lax.broadcasted_iota(jnp.int32, (1, slots_all), 1)
    live = slot < count[0, 0]
    which = lists[2]
    row_hit = jnp.logical_and(
        lax.broadcasted_iota(jnp.int32, (rows, slots_all), 0) == jnp.right_shift(cell, 7), live
    )
    values = [
        jnp.right_shift(which, shift_bits) + 1,
        jnp.bitwise_and(which, slots - 1),
        jnp.right_shift(lists[1], 1),
    ]
    left = jnp.concatenate(
        [jnp.where(row_hit, value.astype(jnp.float32), 0.0) for value in values], axis=0
    ).astype(jnp.bfloat16)
    right = jnp.where(
        lax.broadcasted_iota(jnp.int32, (LANES, slots_all), 0)
        == jnp.bitwise_and(cell, LANES - 1),
        1.0,
        0.0,
    ).astype(jnp.bfloat16)
    table = lax.dot_general(
        left, right, (((1,), (1,)), ((), ())), preferred_element_type=jnp.float32
    )

    for part in range(slots_all // LANES):
        lanes = slice(part * LANES, (part + 1) * LANES)
        cells = stencil[0, 0, :, lanes]
        lane = jnp.bitwise_and(cells, LANES - 1)
        row = jnp.right_shift(cells, 7)
        picked = [jnp.zeros(cells.shape, jnp.float32)] * 3
        for r in range(rows):
            here = row == r
            for c in range(3):
                picked[c] = jnp.where(
                    here, lane_gather(vel[c * rows + r : c * rows + r + 1, :], lane), picked[c]
                )
        factor = weight[0, 0, :, lanes]
        for c in range(3):
            n = part * 3 + c
            samples[n : n + 1, :] = jnp.sum(picked[c] * factor, axis=0, keepdims=True)
    rx_row[my_y] = samples[...]

    def equilibrium_terms(n):
        square = [value * value for value in n]
        return 1.0 - 1.5 * (square[0] + square[1] + square[2])

    def along(n, step):
        total = None
        for c in range(3):
            if step[c] > 0:
                total = plus(total, n[c])
            elif step[c] < 0:
                total = minus(total, n[c])
        return total

    def pairs(rho, n):
        rest = rho * equilibrium_terms(n)
        found = {13: rest}
        rho3, rho45 = (rho * 3.0, rho * 4.5)
        for i in range(13):
            s = along(n, steps[i])
            even = rest + rho45 * s * s
            odd = rho3 * s
            found[i], found[26 - i] = (even + odd, even - odd)
        return found

    coefficient = equilibrium_moments()
    near_rows = [
        ((a + 1) * 3 + c + 1, x)
        for a in (-1, 0, 1)
        for c in (-1, 0, 1)
        for x in range(size_x)
        if 0 <= x + a < size_x
    ]
    ends = ((0, size_x - 1), (1, 0))
    for x in range(size_x):
        found, u = (moments[x], speeds[x])
        ux, uy, uz = u
        rho, mx, my, mz = (found[0], found[9], found[3], found[1])
        owner = table[x * size_y : (x + 1) * size_y]
        place = table[rows + x * size_y : rows + (x + 1) * size_y]
        axis = table[2 * rows + x * size_y : 2 * rows + (x + 1) * size_y]
        held = jnp.where(owner > 0.5, rho, 0.0)
        code = jnp.where(owner > 0.5, (owner - 1.0) * np.float32(slots) + place + 1.0, 0.0)
        marked = solid[x].astype(jnp.float32)
        extra = [held, code, axis, marked]
        for f in range(3):
            fields[f, x] = extra[f]
        basis = [rho, mx, my, mz, mx * ux, my * uy, mz * uz, mx * uy, mx * uz, my * uz]
        deviation = []
        for j in range(27):
            if j in (0, 1, 3, 9):
                deviation.append(None)
            else:
                balance = combine(list(zip(coefficient[j], basis)))
                deviation.append(minus(found[j], balance) * relax[j])
        change = backward(deviation)
        local = pairs(held, u)
        for i in range(27):
            a, b, c = steps[i]
            half = 0.5 ** int(np.sum(steps[i] != 0)) / weights[i]
            value = pop[i, x] - change[i] * np.float32(half) - local[i]
            post[i, x] = value
            for way, edge in ends:
                if x == edge and a == 1 - 2 * way:
                    face[way, (b + 1) * 3 + c + 1] = value
            if b != 0:
                side = 0 if b > 0 else 1
                y = size_y - 1 if b > 0 else 0
                line = value[y : y + 1, :]
                j = (a + 1) * 3 + c + 1
                if (j, x) in near_rows:
                    n = near_rows.index((j, x))
                    near[side, n : n + 1, :] = line
                else:
                    corner[0 if a > 0 else 1, side, c + 1 : c + 2, :] = line
        for way, edge in ends:
            if x == edge:
                for f in range(4):
                    face[way, 9 + f] = extra[f]
        for side, y in ((0, size_y - 1), (1, 0)):
            for f in range(4):
                line = extra[f][y : y + 1, :]
                n = len(near_rows) + f * size_x + x
                near[side, n : n + 1, :] = line
                for way, edge in ends:
                    if x == edge:
                        corner[way, side, 3 + f : 4 + f, :] = line

    def send(src, dst, sem, dx, dy):
        pltpu.make_async_remote_copy(
            src_ref=src,
            dst_ref=dst,
            send_sem=send_sem,
            recv_sem=sem,
            device_id={"gx": dx, "gy": columns[dy]},
            device_id_type=MESH,
        ).start()

    across = sorted(range(devices_y), key=lambda dy: -min(dy, devices_y - dy))
    pl.semaphore_wait(barrier, len(peers))
    first = jnp.where(my_x == 0, 1, 0)
    for step in range(2):
        way = first if step == 0 else 1 - first
        dx = wrap(my_x + 1 - 2 * way, devices_x)
        for dy in across:
            send(samples, rx_x.at[way, my_y], far_sem.at[way], dx, dy)
        for side, dy in ((0, 1), (1, -1)):
            send(corner.at[way, side], got_corner.at[way, side], far_sem.at[way], dx, dy)
        send(face.at[way], got_face.at[way], face_sem.at[way], dx, 0)
        if step == 0:
            for side, dy in ((0, 1), (1, -1)):
                send(near.at[side], got_near.at[side], near_sem, my_x, dy)
            for dy in across:
                if dy != 0:
                    send(samples, rx_row.at[my_y], near_sem, my_x, dy)

    def lookup(code, axis, operand, offset):
        r = code.astype(jnp.int32) - 1
        owner = jnp.right_shift(r, shift_bits)
        lane = jnp.bitwise_and(r, slots - 1) + offset
        value = [jnp.zeros(tile, jnp.float32)] * 3
        for peer in range(devices_y):
            here = owner == peer
            for c in range(3):
                value[c] = jnp.where(
                    here,
                    jnp.take_along_axis(operand(peer, c), lane, axis=1, mode="promise_in_bounds"),
                    value[c],
                )
        return [jnp.where(axis == np.float32(c), 0.0, value[c] * ratio) for c in range(3)]

    def spread(line):
        return jnp.broadcast_to(line, tile)

    def part_of(owner):
        return (owner * slots) // LANES * 3, lax.rem(owner * slots, LANES)

    def mend(value, line, b):
        edge = 0 if b > 0 else size_y - 1
        return jnp.where(row_line == edge, spread(line), value)

    part, offset = part_of(my_y)

    near_count = pltpu.make_async_copy(
        tally.at[0 : (2 * near.shape[1] + (devices_y - 1) * samples.shape[0]) // size_y],
        tally.at[0 : (2 * near.shape[1] + (devices_y - 1) * samples.shape[0]) // size_y],
        near_sem,
    )
    near_count.wait()
    for x in range(size_x):
        n = lookup(
            fields[1, x],
            fields[2, x],
            lambda peer, c: spread(rx_row[peer, pl.ds(part + c, 1), :]),
            offset,
        )
        found = pairs(fields[0, x], n)
        for i in range(27):
            _, b, c = steps[i]
            value = post[i, x] + found[i]
            settled[i, x] = value
            shifted[i, x] = roll(roll(value, b, 0), c, 1)

    for side in range(2):
        for n, (j, x) in enumerate(near_rows):
            q = side * size_x + x
            lines[j, q : q + 1, :] = got_near[side, n : n + 1, :]
        for f in range(4):
            for x in range(size_x):
                n = len(near_rows) + f * size_x + x
                q = side * size_x + x
                lines[9 + f, q : q + 1, :] = got_near[side, n : n + 1, :]
    lower = row_line < size_x
    part0, offset0 = part_of(columns[-1])
    part1, offset1 = part_of(columns[1])
    n = lookup(
        lines[10],
        lines[11],
        lambda peer, c: jnp.where(
            lower,
            spread(rx_row[peer, pl.ds(part0 + c, 1), :]),
            spread(rx_row[peer, pl.ds(part1 + c, 1), :]),
        ),
        jnp.where(lower, offset0, offset1),
    )
    sign_b = jnp.where(lower, 1.0, -1.0)
    n[1] = n[1] * sign_b
    rho = lines[9]
    rest = equilibrium_terms(n)
    border = []
    for j in range(9):
        a, c = (j // 3 - 1, j % 3 - 1)
        s = along(n, (a, 1, c))
        border.append(roll(lines[j] + rho * (rest + s * (3.0 + 4.5 * s)), c, 1))
    marked = [roll(lines[12], c, 1) for c in (-1, 0, 1)]
    for x in range(size_x):
        plane = solid[x].astype(jnp.float32)
        for b in (-1, 0, 1):
            turned = roll(plane, b, 0)
            for c in (-1, 0, 1):
                value = roll(turned, c, 1)
                if b != 0:
                    q = (0 if b > 0 else 1) * size_x + x
                    value = mend(value, marked[c + 1][q : q + 1, :], b)
                masks[(b + 1) * 3 + c + 1, x] = value
    for i in range(27):
        a, b, c = steps[i]
        k = (b + 1) * 3 + c + 1
        for x in range(size_x):
            origin = x - a
            if 0 <= origin < size_x:
                value = shifted[i, origin]
                if b != 0:
                    q = (0 if b > 0 else 1) * size_x + origin
                    value = mend(value, border[(a + 1) * 3 + c + 1][q : q + 1, :], b)
                out[i, x] = jnp.where(masks[k, origin] != 0, settled[26 - i, x], value)

    for way in (1, 0):
        pltpu.make_async_copy(got_face.at[way], got_face.at[way], face_sem.at[way]).wait()
        for k in range(9):
            b, c = (k // 3 - 1, k % 3 - 1)
            moved[way, k] = roll(roll(got_face[way, k], b, 0), c, 1)
            moved[way, 9 + k] = roll(roll(got_face[way, 12], b, 0), c, 1)

    far_tiles = (devices_y * samples.shape[0] + 2 * corner.shape[2]) // size_y
    for way in (1, 0):
        pltpu.make_async_copy(
            tally.at[0:far_tiles], tally.at[0:far_tiles], far_sem.at[way]
        ).wait()

    def stack(line):
        return jnp.where(
            row_line == 0,
            spread(line(0, 0)),
            jnp.where(
                row_line == 1,
                spread(line(0, 1)),
                jnp.where(row_line == 2, spread(line(1, 0)), spread(line(1, 1))),
            ),
        )

    quantity = [stack(lambda way, side: got_corner[way, side, f : f + 1, :]) for f in range(7)]
    even = jnp.bitwise_and(row_line, 1) == 0
    parts = (part0, part1)
    n = lookup(
        quantity[4],
        quantity[5],
        lambda peer, c: stack(lambda way, side: rx_x[way, peer, pl.ds(parts[side] + c, 1), :]),
        jnp.where(even, offset0, offset1),
    )
    rest = equilibrium_terms(n)
    s = jnp.where(row_line < 2, n[0], -n[0]) + jnp.where(even, n[1], -n[1])
    corners, marked = ([], [])
    for c in (-1, 0, 1):
        t = s if c == 0 else s + n[2] if c > 0 else s - n[2]
        value = quantity[c + 1] + quantity[3] * (rest + t * (3.0 + 4.5 * t))
        corners.append(roll(value, c, 1))
        marked.append(roll(quantity[6], c, 1))

    for way, a in ((1, -1), (0, 1)):
        n = lookup(
            got_face[way, 10],
            got_face[way, 11],
            lambda peer, c: spread(rx_x[way, peer, pl.ds(part + c, 1), :]),
            offset,
        )
        rho = got_face[way, 9]
        rest = equilibrium_terms(n)
        x = 0 if a > 0 else size_x - 1
        for k in range(9):
            b, c = (k // 3 - 1, k % 3 - 1)
            i = (a + 1) * 9 + k
            s = along(n, (a, b, c))
            value = moved[way, k] + roll(roll(rho * (rest + s * (3.0 + 4.5 * s)), b, 0), c, 1)
            mark = moved[way, 9 + k]
            if b != 0:
                q = way * 2 + (0 if b > 0 else 1)
                value = mend(value, corners[c + 1][q : q + 1, :], b)
                mark = mend(mark, marked[c + 1][q : q + 1, :], b)
            out[i, x] = jnp.where(mark != 0, settled[26 - i, x], value)
    pltpu.make_async_copy(tally, tally, send_sem).wait()


def write_out(source, out, sem):
    copy = pltpu.make_async_copy(source, out, sem)
    copy.start()
    copy.wait()


def local(populations, relax, solid, wall_cell, wall_normal, wall_count, sample_ref, cells, factors):
    devices_x, devices_y = (lax.axis_size("gx"), lax.axis_size("gy"))
    size_x, size_y, size_z = populations.shape[1:]
    slots_all = wall_cell.shape[2]
    slots = slots_all // devices_y
    assert size_z == LANES and LANES % slots == 0 and slots & (slots - 1) == 0
    assert slots_all % LANES == 0 and devices_x > 2 and devices_y > 2
    assert 1 < size_x and 2 * size_x <= size_y == 8
    f32, i32 = (jnp.float32, jnp.int32)
    near_lines = -(-(9 * size_x - 6 + 4 * size_x) // 8) * 8
    held = -(-3 * slots_all // LANES // 8) * 8
    sent = (3 * devices_y - 1) * held + 2 * 13 * size_y + 2 * near_lines + 4 * 8
    vmem = pltpu.VMEM
    tile = (size_y, LANES)
    anywhere = pl.BlockSpec(memory_space=pl.ANY)
    dma = pltpu.SemaphoreType.DMA
    result = pl.pallas_call(
        functools.partial(kernel, devices_x, devices_y),
        out_shape=pltpu.VMEM(populations.shape, f32),
        in_specs=[anywhere] * 9,
        out_specs=pl.BlockSpec(memory_space=pltpu.VMEM),
        scratch_shapes=[
            vmem(populations.shape, f32),
            pltpu.SMEM(relax.shape, f32),
            pltpu.SMEM(wall_count.shape, i32),
            vmem(solid.shape, i32),
            vmem((3, 1, slots_all), i32),
            vmem(cells.shape, i32),
            vmem(factors.shape, f32),
            vmem((3 * size_x * size_y, LANES), f32),
            vmem((held, LANES), f32),
            vmem((devices_y, held, LANES), f32),
            vmem((2, devices_y, held, LANES), f32),
            vmem(populations.shape, f32),
            vmem(populations.shape, f32),
            vmem(populations.shape, f32),
            vmem((3, size_x) + tile, f32),
            vmem((2, 13) + tile, f32),
            vmem((2, near_lines, LANES), f32),
            vmem((2, 2, 8, LANES), f32),
            vmem((2, 13) + tile, f32),
            vmem((2, near_lines, LANES), f32),
            vmem((2, 2, 8, LANES), f32),
            vmem((13,) + tile, f32),
            vmem((9, size_x) + tile, f32),
            vmem((2, 18) + tile, f32),
            vmem((sent // size_y,) + tile, f32),
            dma((7,)),
            dma,
            dma,
            dma((2,)),
            dma((2,)),
        ],
        compiler_params=pltpu.CompilerParams(collective_id=0, has_side_effects=True),
        name="lattice_step",
    )(populations, relax, solid, wall_cell, wall_normal, wall_count, sample_ref, cells, factors)
    result = pltpu.with_memory_space_constraint(result, pltpu.VMEM)
    return pl.pallas_call(
        write_out,
        out_shape=jax.ShapeDtypeStruct(populations.shape, f32),
        in_specs=[pl.BlockSpec(memory_space=pltpu.VMEM)],
        out_specs=anywhere,
        scratch_shapes=[pltpu.SemaphoreType.DMA],
        name="write_out",
    )(result)


def solution(mesh):
    return jax.shard_map(
        local,
        mesh=mesh,
        in_specs=(
            P(None, "gx", "gy", None),
            P(),
            P("gx", "gy", None),
            P("gx", "gy", None),
            P("gx", "gy", None),
            P("gx", "gy"),
            P("gx", "gy", None),
            P("gx", "gy", None, None),
            P("gx", "gy", None, None),
        ),
        out_specs=P(None, "gx", "gy", None),
        check_vma=False,
    )
```

time: 13.9 us -> 12.3 us (0.88)
  Pallas kernels: 13.1 us -> 11.5 us
    pallas_call x1, Pallas kernels: 12.4 us -> 10.8 us  [local(): pl.pallas_call(functools.partial(kernel, devices_x, devices_y), out_shape...]
where the time goes in v1:
time: 12.3 us; the launch traced here: 12.1 us
  Pallas kernels  11.5 us (93%)
  between operations  0.66 us (5%)
    pallas_call x1, Pallas kernels, local(): pl.pallas_call(functools.partial(kernel, devices_x, devices_y), out_shape...  10.8 us
    pallas_call x1, Pallas kernels, local(): pl.pallas_call(write_out, out_shape=jax.ShapeDtypeStruct(populations.shap...  0.7 us

profile of v1, /device:TPU:0, one launch (start us, length us, event | category | flops | bytes accessed | tf_op | source)
XLA Modules:
  0.0 12.1 jit_solution(1575466963987810725)
XLA Ops:
  0.7 10.8 %lattice_step.1.source = f32[27,2,8,128]{3,2,1,0:T(8,128)S(1)} custom-call(f32[27,2,8,128]{3,2,1,0:T(8,128)} %pop_hbm.1, f32[27]{0:T(128)} %relax_hbm.1, s32[2,8,128]{2,1,0:T(8,128)} %solid_hbm.1, s32[1,1,256]{2,1,0:T(1,128)} %wall_hbm.1, s32[1,1,256]{2,1,0:T(1,128)} %normal_hbm.1, s32[1,1]{1,0:T(1,128)S(6)} %copy.10.count_hbm, s32[1,1,256]{2,1,0:T(1,128)} %ref_hbm.1, ...), custom_call_target="tpu_custom_call" | custom-call | tf_op jit(solution)/shard_map/lattice_step/pallas_call | solution.py:550
  11.4 0.7 %write_out.1 = f32[27,2,8,128]{3,2,1,0:T(8,128)} custom-call(f32[27,2,8,128]{3,2,1,0:T(8,128)S(1)} %lattice_step.1.source), custom_call_target="tpu_custom_call" | custom-call | tf_op jit(solution)/shard_map/write_out/pallas_call | solution.py:591

commit v2 on v1

--- a/solution.py
+++ b/solution.py
@@ -7,6 +7,7 @@
 from jax.experimental import pallas as pl
 from jax.experimental.pallas import tpu as pltpu
 from jax.sharding import PartitionSpec as P
+
 
 steps = np.array([(a - 1, b - 1, c - 1) for a in range(3) for b in range(3) for c in range(3)])
 wall_ratio = (1.0 / 9.0) ** (1.0 / 7.0)
@@ -99,23 +100,17 @@
 def kernel(
     devices_x,
     devices_y,
-    pop_hbm,
-    relax_hbm,
-    solid_hbm,
-    wall_hbm,
-    normal_hbm,
-    count_hbm,
-    ref_hbm,
-    stencil_hbm,
-    weight_hbm,
-    out,
+    gate,
     pop,
     relax,
+    solid,
+    wall,
+    normal,
     count,
-    solid,
-    lists,
+    ref,
     stencil,
     weight,
+    out,
     vel,
     samples,
     rx_row,
@@ -134,15 +129,16 @@
     masks,
     moved,
     tally,
-    load_sem,
     send_sem,
     near_sem,
     face_sem,
     far_sem,
+    row_ready,
+    ready,
 ):
     size_x, size_y = pop.shape[1:3]
     rows = size_x * size_y
-    slots_all = lists.shape[2]
+    slots_all = wall.shape[2]
     slots = slots_all // devices_y
     shift_bits = slots.bit_length() - 1
     my_x = lax.axis_index("gx")
@@ -153,39 +149,36 @@
     def wrap(value, size):
         return jnp.where(value < 0, value + size, jnp.where(value >= size, value - size, value))
 
-    loads = [
-        pltpu.make_async_copy(src, dst, load_sem.at[n])
-        for n, src, dst in [
-            (0, pop_hbm, pop),
-            (1, stencil_hbm, stencil),
-            (2, weight_hbm, weight),
-            (3, wall_hbm.at[0], lists.at[0]),
-            (3, normal_hbm.at[0], lists.at[1]),
-            (3, ref_hbm.at[0], lists.at[2]),
-            (4, count_hbm, count),
-            (5, solid_hbm, solid),
-            (6, relax_hbm, relax),
-        ]
-    ]
-    for load in loads:
-        load.start()
     barrier = pltpu.get_barrier_semaphore()
     columns = {dy: wrap(my_y + dy, devices_y) for dy in range(devices_y)}
     columns[-1] = columns[devices_y - 1]
     beside = {dx: wrap(my_x + dx, devices_x) for dx in (-1, 0, 1)}
-    peers = [(dx, dy) for dx in (-1, 1, 0) for dy in range(devices_y) if (dx, dy) != (0, 0)]
-    for dx, dy in peers:
+    last = devices_x - 1
+    inner = my_y - jnp.bitwise_and(my_y, 1)
+    outer = inner + 2
+    below = jnp.minimum(outer, devices_y)
+
+    def tell(sem, dx, dy):
         pl.semaphore_signal(
-            barrier,
+            sem,
             inc=1,
             device_id={"gx": beside[dx], "gy": columns[dy]},
             device_id_type=MESH,
         )
-    for n in (0, 1, 2):
-        loads[n].wait()
-    pltpu.make_async_copy(lists, lists, load_sem.at[3]).wait()
-    for n in (6, 7, 8):
-        loads[n].wait()
+
+    def when(condition, *signal):
+        pl.when(condition)(lambda: tell(*signal))
+
+    at_last = my_x == last
+    inward = jnp.where(my_x == 0, inner, 0)
+    outward = jnp.where(at_last, devices_y, jnp.where(my_x == last - 1, inner, 0))
+    higher = jnp.where(at_last, devices_y, 2 * devices_y)
+    for dy in range(devices_y):
+        when(columns[dy] >= inward, barrier, -1, dy)
+    for dy in range(devices_y):
+        when(columns[dy] >= outward, barrier, 1, dy)
+    for dy in range(1, devices_y):
+        when(my_y + dy < higher, barrier, 0, dy)
 
     row_line = lax.broadcasted_iota(jnp.int32, tile, 0)
 
@@ -200,17 +193,17 @@
         moments.append(found)
         speeds.append(u)
 
-    cell = lists[0]
+    cell = wall[0]
     slot = lax.broadcasted_iota(jnp.int32, (1, slots_all), 1)
     live = slot < count[0, 0]
-    which = lists[2]
+    which = ref[0]
     row_hit = jnp.logical_and(
         lax.broadcasted_iota(jnp.int32, (rows, slots_all), 0) == jnp.right_shift(cell, 7), live
     )
     values = [
         jnp.right_shift(which, shift_bits) + 1,
         jnp.bitwise_and(which, slots - 1),
-        jnp.right_shift(lists[1], 1),
+        jnp.right_shift(normal[0], 1),
     ]
     left = jnp.concatenate(
         [jnp.where(row_hit, value.astype(jnp.float32), 0.0) for value in values], axis=0
@@ -268,6 +261,7 @@
         return found
 
     coefficient = equilibrium_moments()
+    rates = [jnp.broadcast_to(relax[0:1, j : j + 1], tile) for j in range(27)]
     near_rows = [
         ((a + 1) * 3 + c + 1, x)
         for a in (-1, 0, 1)
@@ -296,7 +290,7 @@
                 deviation.append(None)
             else:
                 balance = combine(list(zip(coefficient[j], basis)))
-                deviation.append(minus(found[j], balance) * relax[j])
+                deviation.append(minus(found[j], balance) * rates[j])
         change = backward(deviation)
         local = pairs(held, u)
         for i in range(27):
@@ -341,22 +335,62 @@
         ).start()
 
     across = sorted(range(devices_y), key=lambda dy: -min(dy, devices_y - dy))
-    pl.semaphore_wait(barrier, len(peers))
-    first = jnp.where(my_x == 0, 1, 0)
-    for step in range(2):
-        way = first if step == 0 else 1 - first
-        dx = wrap(my_x + 1 - 2 * way, devices_x)
+
+    def send_to(way, dy):
+        dx = beside[1 - 2 * way]
+        send(samples, rx_x.at[way, my_y], far_sem.at[way], dx, dy)
+        for side, corner_dy in ((0, 1), (1, devices_y - 1)):
+            if dy == corner_dy:
+                send(corner.at[way, side], got_corner.at[way, side], far_sem.at[way], dx, dy)
+        if dy == 0:
+            send(face.at[way], got_face.at[way], face_sem.at[way], dx, dy)
+
+    def send_all(way):
         for dy in across:
-            send(samples, rx_x.at[way, my_y], far_sem.at[way], dx, dy)
+            send_to(way, dy)
+
+    known = (3 * devices_y - 1) - jnp.where(my_x == 0, devices_y, 0)
+    pl.semaphore_wait(barrier, jnp.where(at_last, my_y + 2 * below, known))
+    answer = jnp.where(at_last, outer, jnp.where(my_x == last - 1, inner, 0))
+    for dy in across:
+        when(columns[dy] < answer, ready, 1, dy)
+
+    def expect(sem, amount):
+        pl.when(amount > 0)(lambda: pl.semaphore_wait(sem, amount))
+
+    def send_near():
         for side, dy in ((0, 1), (1, -1)):
-            send(corner.at[way, side], got_corner.at[way, side], far_sem.at[way], dx, dy)
-        send(face.at[way], got_face.at[way], face_sem.at[way], dx, 0)
-        if step == 0:
-            for side, dy in ((0, 1), (1, -1)):
-                send(near.at[side], got_near.at[side], near_sem, my_x, dy)
-            for dy in across:
-                if dy != 0:
-                    send(samples, rx_row.at[my_y], near_sem, my_x, dy)
+            send(near.at[side], got_near.at[side], near_sem, my_x, dy)
+        for dy in across:
+            if dy != 0:
+                send(samples, rx_row.at[my_y], near_sem, my_x, dy)
+
+    @pl.when(at_last)
+    def _():
+        for dy in across:
+            pl.when(columns[dy] < outer)(lambda dy=dy: send_to(0, dy))
+        for dy in range(1, devices_y):
+            when(my_y + dy >= devices_y, row_ready, 0, dy)
+        expect(row_ready, devices_y - 1 - my_y)
+        for dy in across:
+
+            @pl.when(columns[dy] >= outer)
+            def _(dy=dy):
+                tell(ready, 1, dy)
+                send_to(0, dy)
+
+        send_near()
+        expect(ready, devices_y - below)
+        send_all(1)
+
+    @pl.when(my_x < last)
+    def _():
+        send_near()
+        send_all(0)
+
+        @pl.when(my_x > 0)
+        def _():
+            send_all(1)
 
     def lookup(code, axis, operand, offset):
         r = code.astype(jnp.int32) - 1
@@ -459,6 +493,11 @@
                     value = mend(value, border[(a + 1) * 3 + c + 1][q : q + 1, :], b)
                 out[i, x] = jnp.where(masks[k, origin] != 0, settled[26 - i, x], value)
 
+    @pl.when(my_x == 0)
+    def _():
+        pl.semaphore_wait(ready, devices_y)
+        send_all(1)
+
     for way in (1, 0):
         pltpu.make_async_copy(got_face.at[way], got_face.at[way], face_sem.at[way]).wait()
         for k in range(9):
@@ -531,6 +570,10 @@
     copy.wait()
 
 
+def pause(out):
+    out[...] = jnp.zeros_like(out)
+
+
 def local(populations, relax, solid, wall_cell, wall_normal, wall_count, sample_ref, cells, factors):
     devices_x, devices_y = (lax.axis_size("gx"), lax.axis_size("gy"))
     size_x, size_y, size_z = populations.shape[1:]
@@ -539,27 +582,34 @@
     assert size_z == LANES and LANES % slots == 0 and slots & (slots - 1) == 0
     assert slots_all % LANES == 0 and devices_x > 2 and devices_y > 2
     assert 1 < size_x and 2 * size_x <= size_y == 8
-    f32, i32 = (jnp.float32, jnp.int32)
+    f32 = jnp.float32
     near_lines = -(-(9 * size_x - 6 + 4 * size_x) // 8) * 8
     held = -(-3 * slots_all // LANES // 8) * 8
     sent = (3 * devices_y - 1) * held + 2 * 13 * size_y + 2 * near_lines + 4 * 8
     vmem = pltpu.VMEM
     tile = (size_y, LANES)
     anywhere = pl.BlockSpec(memory_space=pl.ANY)
+    on_core = pl.BlockSpec(memory_space=pltpu.VMEM)
+    scalars = pl.BlockSpec(memory_space=pltpu.SMEM)
+
+    def near_core(value):
+        return pltpu.with_memory_space_constraint(value, pltpu.VMEM)
+
     dma = pltpu.SemaphoreType.DMA
+    regular = pltpu.SemaphoreType.REGULAR
+    gate = pl.pallas_call(
+        pause,
+        out_shape=pltpu.VMEM(tile, f32),
+        out_specs=pl.BlockSpec(memory_space=pltpu.VMEM),
+        cost_estimate=pl.CostEstimate(flops=10**9, bytes_accessed=4096, transcendentals=0),
+        name="pause",
+    )()
     result = pl.pallas_call(
         functools.partial(kernel, devices_x, devices_y),
         out_shape=pltpu.VMEM(populations.shape, f32),
-        in_specs=[anywhere] * 9,
+        in_specs=[on_core] * 6 + [scalars] + [on_core] * 3,
         out_specs=pl.BlockSpec(memory_space=pltpu.VMEM),
         scratch_shapes=[
-            vmem(populations.shape, f32),
-            pltpu.SMEM(relax.shape, f32),
-            pltpu.SMEM(wall_count.shape, i32),
-            vmem(solid.shape, i32),
-            vmem((3, 1, slots_all), i32),
-            vmem(cells.shape, i32),
-            vmem(factors.shape, f32),
             vmem((3 * size_x * size_y, LANES), f32),
             vmem((held, LANES), f32),
             vmem((devices_y, held, LANES), f32),
@@ -578,15 +628,27 @@
             vmem((9, size_x) + tile, f32),
             vmem((2, 18) + tile, f32),
             vmem((sent // size_y,) + tile, f32),
-            dma((7,)),
             dma,
             dma,
             dma((2,)),
             dma((2,)),
+            regular,
+            regular,
         ],
         compiler_params=pltpu.CompilerParams(collective_id=0, has_side_effects=True),
         name="lattice_step",
-    )(populations, relax, solid, wall_cell, wall_normal, wall_count, sample_ref, cells, factors)
+    )(
+        pltpu.with_memory_space_constraint(gate, pltpu.VMEM),
+        near_core(populations),
+        near_core(relax.reshape(1, 27)),
+        near_core(solid),
+        near_core(wall_cell),
+        near_core(wall_normal),
+        wall_count,
+        near_core(sample_ref),
+        near_core(cells),
+        near_core(factors),
+    )
     result = pltpu.with_memory_space_constraint(result, pltpu.VMEM)
     return pl.pallas_call(
         write_out,

time: 12.3 us -> 12.8 us (1.041)
  local copies, waits for them, and re-layouts: 0 us -> 0.88 us
  Pallas kernels: 11.5 us -> 11 us
    unnamed x0 -> x16, local copies, waits for them, and re-layouts: none -> 0.88 us
    pallas_call x1, Pallas kernels: 10.8 us -> 10.3 us  [local(): pl.pallas_call(functools.partial(kernel, devices_x, devices_y), out_shape...]
where the time goes in v2:
time: 12.8 us; the launch traced here: 12.6 us
  Pallas kernels  11 us (86%)
  local copies, waits for them, and re-layouts  0.88 us (7%)
  between operations  0.76 us (6%)
    pallas_call x1, Pallas kernels, local(): pl.pallas_call(functools.partial(kernel, devices_x, devices_y), out_shape...  10.3 us
    unnamed x16, local copies, waits for them, and re-layouts  0.88 us
    pallas_call x1, Pallas kernels, local(): pl.pallas_call(write_out, out_shape=jax.ShapeDtypeStruct(populations.shap...  0.7 us

profile of v2, /device:TPU:0, one launch (start us, length us, event | category | flops | bytes accessed | tf_op | source)
XLA Modules:
  0.0 12.6 jit_solution(16608932559183058438)
XLA Ops:
  0.7 0.0 copy-start
  0.7 0.0 copy-start.1
  0.7 0.0 copy-start.2
  0.7 0.0 copy-start.3
  0.7 0.0 copy-start.4
  0.7 0.0 copy-start.5
  0.7 0.0 copy-start.6
  0.7 0.0 copy-start.7
  0.7 0.8 %copy-done = f32[27,2,8,128]{3,2,1,0:T(8,128)S(1)} copy-done((f32[27,2,8,128]{3,2,1,0:T(8,128)S(1)}, f32[27,2,8,128]{3,2,1,0:T(8,128)}, u32[]{:S(2)}) %copy-start) | copy-done | bytes 221208
  1.6 0.0 copy-done.1
  1.6 0.0 copy-done.2
  1.6 0.0 copy-done.3
  1.6 0.0 copy-done.4
  1.6 0.0 copy-done.5
  1.6 0.0 copy-done.6
  1.6 0.0 copy-done.7
  1.6 10.3 %lattice_step.1.source = f32[27,2,8,128]{3,2,1,0:T(8,128)S(1)} custom-call(f32[8,128]{1,0:T(8,128)S(1)} %pause.1.gate, f32[27,2,8,128]{3,2,1,0:T(8,128)S(1)} %copy-done, f32[1,27]{1,0:T(1,128)S(1)} %bitcast.1, s32[2,8,128]{2,1,0:T(8,128)S(1)} %copy-done.1, s32[1,1,256]{2,1,0:T(1,128)S(1)} %copy-done.4, s32[1,1,256]{2,1,0:T(1,128)S(1)} %copy-done.5, ...), custom_call_target="tpu_custom_call" | custom-call | tf_op jit(solution)/shard_map/lattice_step/pallas_call | solution.py:607
  11.9 0.7 %write_out.1 = f32[27,2,8,128]{3,2,1,0:T(8,128)} custom-call(f32[27,2,8,128]{3,2,1,0:T(8,128)S(1)} %lattice_step.1.source), custom_call_target="tpu_custom_call" | custom-call | tf_op jit(solution)/shard_map/write_out/pallas_call | solution.py:653
  (1 shorter events, 0.0 us)
Async XLA Ops:
  0.7 0.9 %copy-start = (f32[27,2,8,128]{3,2,1,0:T(8,128)S(1)}, f32[27,2,8,128]{3,2,1,0:T(8,128)}, u32[]{:S(2)}) copy-start(f32[27,2,8,128]{3,2,1,0:T(8,128)} %pop.1) | copy-start | bytes 663556
  0.7 0.9 %copy-start.1 = (s32[2,8,128]{2,1,0:T(8,128)S(1)}, s32[2,8,128]{2,1,0:T(8,128)}, u32[]{:S(2)}) copy-start(s32[2,8,128]{2,1,0:T(8,128)} %solid.1) | copy-start | bytes 24580
  0.7 0.9 %copy-start.2 = (s32[1,1,8,256]{3,2,1,0:T(8,128)S(1)}, s32[1,1,8,256]{3,2,1,0:T(8,128)}, u32[]{:S(2)}) copy-start(s32[1,1,8,256]{3,2,1,0:T(8,128)} %stencil.1) | copy-start | bytes 24580
  0.7 0.9 %copy-start.3 = (f32[1,1,8,256]{3,2,1,0:T(8,128)S(1)}, f32[1,1,8,256]{3,2,1,0:T(8,128)}, u32[]{:S(2)}) copy-start(f32[1,1,8,256]{3,2,1,0:T(8,128)} %weight.1) | copy-start | bytes 24580
  0.7 0.9 %copy-start.4 = (s32[1,1,256]{2,1,0:T(1,128)S(1)}, s32[1,1,256]{2,1,0:T(1,128)}, u32[]{:S(2)}) copy-start(s32[1,1,256]{2,1,0:T(1,128)} %wall.1) | copy-start | bytes 3076
  0.7 0.9 %copy-start.5 = (s32[1,1,256]{2,1,0:T(1,128)S(1)}, s32[1,1,256]{2,1,0:T(1,128)}, u32[]{:S(2)}) copy-start(s32[1,1,256]{2,1,0:T(1,128)} %normal.1) | copy-start | bytes 3076
  0.7 0.9 %copy-start.6 = (s32[1,1,256]{2,1,0:T(1,128)S(1)}, s32[1,1,256]{2,1,0:T(1,128)}, u32[]{:S(2)}) copy-start(s32[1,1,256]{2,1,0:T(1,128)} %ref.1) | copy-start | bytes 3076
  0.7 0.9 %copy-start.7 = (f32[27]{0:T(128)S(1)}, f32[27]{0:T(128)}, u32[]{:S(2)}) copy-start(f32[27]{0:T(128)} %param.10) | copy-start | bytes 328

commit v3 on v2

--- a/solution.py
+++ b/solution.py
@@ -134,6 +134,7 @@
     face_sem,
     far_sem,
     row_ready,
+    cross,
     ready,
 ):
     size_x, size_y = pop.shape[1:3]
@@ -170,15 +171,14 @@
         pl.when(condition)(lambda: tell(*signal))
 
     at_last = my_x == last
-    inward = jnp.where(my_x == 0, inner, 0)
-    outward = jnp.where(at_last, devices_y, jnp.where(my_x == last - 1, inner, 0))
-    higher = jnp.where(at_last, devices_y, 2 * devices_y)
+    inward = jnp.where(my_x == 0, inner, devices_y)
+    outward = jnp.where(at_last, devices_y, inner)
     for dy in range(devices_y):
         when(columns[dy] >= inward, barrier, -1, dy)
     for dy in range(devices_y):
         when(columns[dy] >= outward, barrier, 1, dy)
     for dy in range(1, devices_y):
-        when(my_y + dy < higher, barrier, 0, dy)
+        when(my_y + dy < devices_y, barrier, 0, dy)
 
     row_line = lax.broadcasted_iota(jnp.int32, tile, 0)
 
@@ -336,61 +336,80 @@
 
     across = sorted(range(devices_y), key=lambda dy: -min(dy, devices_y - dy))
 
+    used = 3 * slots_all // LANES
+
     def send_to(way, dy):
-        dx = beside[1 - 2 * way]
-        send(samples, rx_x.at[way, my_y], far_sem.at[way], dx, dy)
+        dx = wrap(my_x + 1 - 2 * way, devices_x)
+        send(samples.at[0:used], rx_x.at[way, my_y, 0:used], far_sem.at[way], dx, dy)
         for side, corner_dy in ((0, 1), (1, devices_y - 1)):
             if dy == corner_dy:
                 send(corner.at[way, side], got_corner.at[way, side], far_sem.at[way], dx, dy)
         if dy == 0:
             send(face.at[way], got_face.at[way], face_sem.at[way], dx, dy)
 
-    def send_all(way):
-        for dy in across:
-            send_to(way, dy)
-
-    known = (3 * devices_y - 1) - jnp.where(my_x == 0, devices_y, 0)
-    pl.semaphore_wait(barrier, jnp.where(at_last, my_y + 2 * below, known))
-    answer = jnp.where(at_last, outer, jnp.where(my_x == last - 1, inner, 0))
-    for dy in across:
-        when(columns[dy] < answer, ready, 1, dy)
-
     def expect(sem, amount):
         pl.when(amount > 0)(lambda: pl.semaphore_wait(sem, amount))
+
+    def both(first, second):
+        return jnp.logical_and(first, second)
 
     def send_near():
         for side, dy in ((0, 1), (1, -1)):
             send(near.at[side], got_near.at[side], near_sem, my_x, dy)
         for dy in across:
             if dy != 0:
-                send(samples, rx_row.at[my_y], near_sem, my_x, dy)
-
-    @pl.when(at_last)
+                send(samples.at[0:used], rx_row.at[my_y, 0:used], near_sem, my_x, dy)
+
+    def send_where(way, chosen):
+        for dy in across:
+            pl.when(chosen[dy])(lambda dy=dy: send_to(way, dy))
+
+    inside = {dy: columns[dy] < outer for dy in across}
+    beyond = {dy: columns[dy] >= outer for dy in across}
+    beneath = {dy: both(columns[dy] >= inner, columns[dy] < outer) for dy in across}
+    top = devices_y - 2
+    low = my_y < top
+    ahead = [(at_last, 1, 0, 0), (my_x > 0, -1, 1, 2)]
+    expect(
+        barrier,
+        my_y + jnp.where(my_x > 0, below, 0) + jnp.where(at_last, below, 0),
+    )
+    for applies, dx, way, n in ahead:
+
+        @pl.when(applies)
+        def _(dx=dx, way=way, n=n):
+            for dy in across:
+                when(beneath[dy], ready.at[n], dx, dy)
+                when(columns[dy] < inner, ready.at[n + 1], dx, dy)
+            send_where(way, inside)
+
+    for dy in range(1, devices_y):
+        crossing = both(jnp.logical_not(low), columns[dy] < top) if dy % 2 == 0 else None
+        lower = my_y + dy >= devices_y
+        if crossing is None:
+            when(lower, row_ready, 0, dy)
+        else:
+            when(crossing, cross, 0, dy)
+            when(both(lower, jnp.logical_not(crossing)), row_ready, 0, dy)
+
+    @pl.when(low)
     def _():
-        for dy in across:
-            pl.when(columns[dy] < outer)(lambda dy=dy: send_to(0, dy))
-        for dy in range(1, devices_y):
-            when(my_y + dy >= devices_y, row_ready, 0, dy)
-        expect(row_ready, devices_y - 1 - my_y)
-        for dy in across:
-
-            @pl.when(columns[dy] >= outer)
-            def _(dy=dy):
-                tell(ready, 1, dy)
-                send_to(0, dy)
-
-        send_near()
-        expect(ready, devices_y - below)
-        send_all(1)
+        pl.semaphore_wait(cross, 1)
+        for applies, dx, way, n in ahead:
+
+            @pl.when(applies)
+            def _(way=way):
+                send_where(way, beyond)
+
+    expect(row_ready, devices_y - 1 - my_y - jnp.where(low, 1, 0))
+    send_near()
 
     @pl.when(my_x < last)
     def _():
-        send_near()
-        send_all(0)
-
-        @pl.when(my_x > 0)
-        def _():
-            send_all(1)
+        pl.semaphore_wait(ready.at[2], below - inner)
+        send_where(0, inside)
+        expect(ready.at[3], devices_y - below)
+        send_where(0, beyond)
 
     def lookup(code, axis, operand, offset):
         r = code.astype(jnp.int32) - 1
@@ -419,9 +438,10 @@
 
     part, offset = part_of(my_y)
 
+    near_total = 2 * near.shape[1] + (devices_y - 1) * used
     near_count = pltpu.make_async_copy(
-        tally.at[0 : (2 * near.shape[1] + (devices_y - 1) * samples.shape[0]) // size_y],
-        tally.at[0 : (2 * near.shape[1] + (devices_y - 1) * samples.shape[0]) // size_y],
+        tally.at[0 : near_total],
+        tally.at[0 : near_total],
         near_sem,
     )
     near_count.wait()
@@ -495,8 +515,10 @@
 
     @pl.when(my_x == 0)
     def _():
-        pl.semaphore_wait(ready, devices_y)
-        send_all(1)
+        pl.semaphore_wait(ready.at[0], below - inner)
+        send_where(1, inside)
+        expect(ready.at[1], devices_y - below)
+        send_where(1, beyond)
 
     for way in (1, 0):
         pltpu.make_async_copy(got_face.at[way], got_face.at[way], face_sem.at[way]).wait()
@@ -505,10 +527,10 @@
             moved[way, k] = roll(roll(got_face[way, k], b, 0), c, 1)
             moved[way, 9 + k] = roll(roll(got_face[way, 12], b, 0), c, 1)
 
-    far_tiles = (devices_y * samples.shape[0] + 2 * corner.shape[2]) // size_y
+    far_total = devices_y * used + 2 * corner.shape[2]
     for way in (1, 0):
         pltpu.make_async_copy(
-            tally.at[0:far_tiles], tally.at[0:far_tiles], far_sem.at[way]
+            tally.at[0:far_total], tally.at[0:far_total], far_sem.at[way]
         ).wait()
 
     def stack(line):
@@ -581,11 +603,13 @@
     slots = slots_all // devices_y
     assert size_z == LANES and LANES % slots == 0 and slots & (slots - 1) == 0
     assert slots_all % LANES == 0 and devices_x > 2 and devices_y > 2
+    assert devices_y % 2 == 0
     assert 1 < size_x and 2 * size_x <= size_y == 8
     f32 = jnp.float32
     near_lines = -(-(9 * size_x - 6 + 4 * size_x) // 8) * 8
     held = -(-3 * slots_all // LANES // 8) * 8
-    sent = (3 * devices_y - 1) * held + 2 * 13 * size_y + 2 * near_lines + 4 * 8
+    used = 3 * slots_all // LANES
+    sent = (3 * devices_y - 1) * used + 2 * 13 * size_y + 2 * near_lines + 4 * 8
     vmem = pltpu.VMEM
     tile = (size_y, LANES)
     anywhere = pl.BlockSpec(memory_space=pl.ANY)
@@ -627,13 +651,14 @@
             vmem((13,) + tile, f32),
             vmem((9, size_x) + tile, f32),
             vmem((2, 18) + tile, f32),
-            vmem((sent // size_y,) + tile, f32),
+            vmem((sent, LANES), f32),
             dma,
             dma,
             dma((2,)),
             dma((2,)),
             regular,
             regular,
+            regular((4,)),
         ],
         compiler_params=pltpu.CompilerParams(collective_id=0, has_side_effects=True),
         name="lattice_step",

time: 12.8 us -> 12 us (0.938)
  Pallas kernels: 11 us -> 10.2 us
    pallas_call x1, Pallas kernels: 10.3 us -> 9.51 us  [local(): pl.pallas_call(functools.partial(kernel, devices_x, devices_y), out_shape...]
where the time goes in v3:
time: 12 us; the launch traced here: 11.9 us
  Pallas kernels  10.2 us (85%)
  local copies, waits for them, and re-layouts  0.88 us (7%)
  between operations  0.76 us (6%)
    pallas_call x1, Pallas kernels, local(): pl.pallas_call(functools.partial(kernel, devices_x, devices_y), out_shape...  9.51 us
    unnamed x16, local copies, waits for them, and re-layouts  0.88 us
    pallas_call x1, Pallas kernels, local(): pl.pallas_call(write_out, out_shape=jax.ShapeDtypeStruct(populations.shap...  0.7 us

profile of v3, /device:TPU:0, one launch (start us, length us, event | category | flops | bytes accessed | tf_op | source)
XLA Modules:
  0.0 11.9 jit_solution(507967554163800022)
XLA Ops:
  0.7 0.0 copy-start
  0.7 0.0 copy-start.1
  0.7 0.0 copy-start.2
  0.7 0.0 copy-start.3
  0.7 0.0 copy-start.4
  0.7 0.0 copy-start.5
  0.7 0.0 copy-start.6
  0.7 0.0 copy-start.7
  0.7 0.8 %copy-done = f32[27,2,8,128]{3,2,1,0:T(8,128)S(1)} copy-done((f32[27,2,8,128]{3,2,1,0:T(8,128)S(1)}, f32[27,2,8,128]{3,2,1,0:T(8,128)}, u32[]{:S(2)}) %copy-start) | copy-done | bytes 221208
  1.6 0.0 copy-done.1
  1.6 0.0 copy-done.2
  1.6 0.0 copy-done.3
  1.6 0.0 copy-done.4
  1.6 0.0 copy-done.5
  1.6 0.0 copy-done.6
  1.6 0.0 copy-done.7
  1.6 9.5 %lattice_step.1.source = f32[27,2,8,128]{3,2,1,0:T(8,128)S(1)} custom-call(f32[8,128]{1,0:T(8,128)S(1)} %pause.1.gate, f32[27,2,8,128]{3,2,1,0:T(8,128)S(1)} %copy-done, f32[1,27]{1,0:T(1,128)S(1)} %bitcast.1, s32[2,8,128]{2,1,0:T(8,128)S(1)} %copy-done.1, s32[1,1,256]{2,1,0:T(1,128)S(1)} %copy-done.4, s32[1,1,256]{2,1,0:T(1,128)S(1)} %copy-done.5, ...), custom_call_target="tpu_custom_call" | custom-call | tf_op jit(solution)/shard_map/lattice_step/pallas_call | solution.py:631
  11.2 0.7 %write_out.1 = f32[27,2,8,128]{3,2,1,0:T(8,128)} custom-call(f32[27,2,8,128]{3,2,1,0:T(8,128)S(1)} %lattice_step.1.source), custom_call_target="tpu_custom_call" | custom-call | tf_op jit(solution)/shard_map/write_out/pallas_call | solution.py:678
  (1 shorter events, 0.0 us)
Async XLA Ops:
  0.7 0.9 %copy-start = (f32[27,2,8,128]{3,2,1,0:T(8,128)S(1)}, f32[27,2,8,128]{3,2,1,0:T(8,128)}, u32[]{:S(2)}) copy-start(f32[27,2,8,128]{3,2,1,0:T(8,128)} %pop.1) | copy-start | bytes 663556
  0.7 0.9 %copy-start.1 = (s32[2,8,128]{2,1,0:T(8,128)S(1)}, s32[2,8,128]{2,1,0:T(8,128)}, u32[]{:S(2)}) copy-start(s32[2,8,128]{2,1,0:T(8,128)} %solid.1) | copy-start | bytes 24580
  0.7 0.9 %copy-start.2 = (s32[1,1,8,256]{3,2,1,0:T(8,128)S(1)}, s32[1,1,8,256]{3,2,1,0:T(8,128)}, u32[]{:S(2)}) copy-start(s32[1,1,8,256]{3,2,1,0:T(8,128)} %stencil.1) | copy-start | bytes 24580
  0.7 0.9 %copy-start.3 = (f32[1,1,8,256]{3,2,1,0:T(8,128)S(1)}, f32[1,1,8,256]{3,2,1,0:T(8,128)}, u32[]{:S(2)}) copy-start(f32[1,1,8,256]{3,2,1,0:T(8,128)} %weight.1) | copy-start | bytes 24580
  0.7 0.9 %copy-start.4 = (s32[1,1,256]{2,1,0:T(1,128)S(1)}, s32[1,1,256]{2,1,0:T(1,128)}, u32[]{:S(2)}) copy-start(s32[1,1,256]{2,1,0:T(1,128)} %wall.1) | copy-start | bytes 3076
  0.7 0.9 %copy-start.5 = (s32[1,1,256]{2,1,0:T(1,128)S(1)}, s32[1,1,256]{2,1,0:T(1,128)}, u32[]{:S(2)}) copy-start(s32[1,1,256]{2,1,0:T(1,128)} %normal.1) | copy-start | bytes 3076
  0.7 0.9 %copy-start.6 = (s32[1,1,256]{2,1,0:T(1,128)S(1)}, s32[1,1,256]{2,1,0:T(1,128)}, u32[]{:S(2)}) copy-start(s32[1,1,256]{2,1,0:T(1,128)} %ref.1) | copy-start | bytes 3076
  0.7 0.9 %copy-start.7 = (f32[27]{0:T(128)S(1)}, f32[27]{0:T(128)}, u32[]{:S(2)}) copy-start(f32[27]{0:T(128)} %param.10) | copy-start | bytes 328

commit v4 on v3

--- a/solution.py
+++ b/solution.py
@@ -173,9 +173,10 @@
     at_last = my_x == last
     inward = jnp.where(my_x == 0, inner, devices_y)
     outward = jnp.where(at_last, devices_y, inner)
-    for dy in range(devices_y):
+    across = sorted(range(devices_y), key=lambda dy: -min(dy, devices_y - dy))
+    for dy in across:
         when(columns[dy] >= inward, barrier, -1, dy)
-    for dy in range(devices_y):
+    for dy in across:
         when(columns[dy] >= outward, barrier, 1, dy)
     for dy in range(1, devices_y):
         when(my_y + dy < devices_y, barrier, 0, dy)
@@ -334,7 +335,6 @@
             device_id_type=MESH,
         ).start()
 
-    across = sorted(range(devices_y), key=lambda dy: -min(dy, devices_y - dy))
 
     used = 3 * slots_all // LANES
 
@@ -378,10 +378,13 @@
 
         @pl.when(applies)
         def _(dx=dx, way=way, n=n):
+            if way == 0:
+                send_where(way, inside)
             for dy in across:
                 when(beneath[dy], ready.at[n], dx, dy)
                 when(columns[dy] < inner, ready.at[n + 1], dx, dy)
-            send_where(way, inside)
+            if way == 1:
+                send_where(way, inside)
 
     for dy in range(1, devices_y):
         crossing = both(jnp.logical_not(low), columns[dy] < top) if dy % 2 == 0 else None
@@ -411,10 +414,11 @@
         expect(ready.at[3], devices_y - below)
         send_where(0, beyond)
 
-    def lookup(code, axis, operand, offset):
+    def decode(code, offset):
         r = code.astype(jnp.int32) - 1
-        owner = jnp.right_shift(r, shift_bits)
-        lane = jnp.bitwise_and(r, slots - 1) + offset
+        return jnp.right_shift(r, shift_bits), jnp.bitwise_and(r, slots - 1) + offset
+
+    def lookup(owner, lane, axis, operand):
         value = [jnp.zeros(tile, jnp.float32)] * 3
         for peer in range(devices_y):
             here = owner == peer
@@ -447,10 +451,9 @@
     near_count.wait()
     for x in range(size_x):
         n = lookup(
-            fields[1, x],
+            *decode(fields[1, x], offset),
             fields[2, x],
             lambda peer, c: spread(rx_row[peer, pl.ds(part + c, 1), :]),
-            offset,
         )
         found = pairs(fields[0, x], n)
         for i in range(27):
@@ -472,14 +475,13 @@
     part0, offset0 = part_of(columns[-1])
     part1, offset1 = part_of(columns[1])
     n = lookup(
-        lines[10],
+        *decode(lines[10], jnp.where(lower, offset0, offset1)),
         lines[11],
         lambda peer, c: jnp.where(
             lower,
             spread(rx_row[peer, pl.ds(part0 + c, 1), :]),
             spread(rx_row[peer, pl.ds(part1 + c, 1), :]),
         ),
-        jnp.where(lower, offset0, offset1),
     )
     sign_b = jnp.where(lower, 1.0, -1.0)
     n[1] = n[1] * sign_b
@@ -520,54 +522,46 @@
         expect(ready.at[1], devices_y - below)
         send_where(1, beyond)
 
-    for way in (1, 0):
+    upper = row_line == 0
+    sideways = jnp.where(upper, offset0, offset1)
+
+    def stack(one, other):
+        return jnp.where(upper, spread(one), spread(other))
+
+    far_total = devices_y * used + 2 * corner.shape[2]
+    for way, a in ((1, -1), (0, 1)):
         pltpu.make_async_copy(got_face.at[way], got_face.at[way], face_sem.at[way]).wait()
         for k in range(9):
             b, c = (k // 3 - 1, k % 3 - 1)
             moved[way, k] = roll(roll(got_face[way, k], b, 0), c, 1)
             moved[way, 9 + k] = roll(roll(got_face[way, 12], b, 0), c, 1)
-
-    far_total = devices_y * used + 2 * corner.shape[2]
-    for way in (1, 0):
+        found_at = decode(got_face[way, 10], offset)
         pltpu.make_async_copy(
             tally.at[0:far_total], tally.at[0:far_total], far_sem.at[way]
         ).wait()
-
-    def stack(line):
-        return jnp.where(
-            row_line == 0,
-            spread(line(0, 0)),
-            jnp.where(
-                row_line == 1,
-                spread(line(0, 1)),
-                jnp.where(row_line == 2, spread(line(1, 0)), spread(line(1, 1))),
+        quantity = [
+            stack(got_corner[way, 0, f : f + 1, :], got_corner[way, 1, f : f + 1, :])
+            for f in range(7)
+        ]
+        n = lookup(
+            *decode(quantity[4], sideways),
+            quantity[5],
+            lambda peer, c: stack(
+                rx_x[way, peer, pl.ds(part0 + c, 1), :], rx_x[way, peer, pl.ds(part1 + c, 1), :]
             ),
         )
-
-    quantity = [stack(lambda way, side: got_corner[way, side, f : f + 1, :]) for f in range(7)]
-    even = jnp.bitwise_and(row_line, 1) == 0
-    parts = (part0, part1)
-    n = lookup(
-        quantity[4],
-        quantity[5],
-        lambda peer, c: stack(lambda way, side: rx_x[way, peer, pl.ds(parts[side] + c, 1), :]),
-        jnp.where(even, offset0, offset1),
-    )
-    rest = equilibrium_terms(n)
-    s = jnp.where(row_line < 2, n[0], -n[0]) + jnp.where(even, n[1], -n[1])
-    corners, marked = ([], [])
-    for c in (-1, 0, 1):
-        t = s if c == 0 else s + n[2] if c > 0 else s - n[2]
-        value = quantity[c + 1] + quantity[3] * (rest + t * (3.0 + 4.5 * t))
-        corners.append(roll(value, c, 1))
-        marked.append(roll(quantity[6], c, 1))
-
-    for way, a in ((1, -1), (0, 1)):
+        n[1] = jnp.where(upper, n[1], -n[1])
+        rest = equilibrium_terms(n)
+        corners, marked = ([], [])
+        for c in (-1, 0, 1):
+            s = along(n, (a, 1, c))
+            value = quantity[c + 1] + quantity[3] * (rest + s * (3.0 + 4.5 * s))
+            corners.append(roll(value, c, 1))
+            marked.append(roll(quantity[6], c, 1))
         n = lookup(
-            got_face[way, 10],
+            *found_at,
             got_face[way, 11],
             lambda peer, c: spread(rx_x[way, peer, pl.ds(part + c, 1), :]),
-            offset,
         )
         rho = got_face[way, 9]
         rest = equilibrium_terms(n)
@@ -579,17 +573,11 @@
             value = moved[way, k] + roll(roll(rho * (rest + s * (3.0 + 4.5 * s)), b, 0), c, 1)
             mark = moved[way, 9 + k]
             if b != 0:
-                q = way * 2 + (0 if b > 0 else 1)
+                q = 0 if b > 0 else 1
                 value = mend(value, corners[c + 1][q : q + 1, :], b)
                 mark = mend(mark, marked[c + 1][q : q + 1, :], b)
             out[i, x] = jnp.where(mark != 0, settled[26 - i, x], value)
     pltpu.make_async_copy(tally, tally, send_sem).wait()
-
-
-def write_out(source, out, sem):
-    copy = pltpu.make_async_copy(source, out, sem)
-    copy.start()
-    copy.wait()
 
 
 def pause(out):
@@ -612,7 +600,6 @@
     sent = (3 * devices_y - 1) * used + 2 * 13 * size_y + 2 * near_lines + 4 * 8
     vmem = pltpu.VMEM
     tile = (size_y, LANES)
-    anywhere = pl.BlockSpec(memory_space=pl.ANY)
     on_core = pl.BlockSpec(memory_space=pltpu.VMEM)
     scalars = pl.BlockSpec(memory_space=pltpu.SMEM)
 
@@ -674,15 +661,7 @@
         near_core(cells),
         near_core(factors),
     )
-    result = pltpu.with_memory_space_constraint(result, pltpu.VMEM)
-    return pl.pallas_call(
-        write_out,
-        out_shape=jax.ShapeDtypeStruct(populations.shape, f32),
-        in_specs=[pl.BlockSpec(memory_space=pltpu.VMEM)],
-        out_specs=anywhere,
-        scratch_shapes=[pltpu.SemaphoreType.DMA],
-        name="write_out",
-    )(result)
+    return pltpu.with_memory_space_constraint(result, pltpu.VMEM)
 
 
 def solution(mesh):

time: 12 us -> 11.9 us (level)
  Pallas kernels: 10.2 us -> 9.46 us
  local copies, waits for them, and re-layouts: 0.88 us -> 1.57 us
    pallas_call x1 -> x0, Pallas kernels: 0.7 us -> none  [local(): pl.pallas_call(write_out, out_shape=jax.ShapeDtypeStruct(populations.shap...]
    unnamed x16 -> x17, local copies, waits for them, and re-layouts: 0.88 us -> 1.57 us
where the time goes in v4:
time: 11.9 us; the launch traced here: 11.8 us
  Pallas kernels  9.46 us (79%)
  local copies, waits for them, and re-layouts  1.57 us (13%)
  between operations  0.76 us (6%)
    pallas_call x1, Pallas kernels, local(): pl.pallas_call(functools.partial(kernel, devices_x, devices_y), out_shape...  9.46 us
    unnamed x17, local copies, waits for them, and re-layouts  1.57 us

profile of v4, /device:TPU:0, one launch (start us, length us, event | category | flops | bytes accessed | tf_op | source)
XLA Modules:
  0.0 11.8 jit_solution(9215410826284940693)
XLA Ops:
  0.7 0.0 copy-start
  0.7 0.0 copy-start.1
  0.7 0.0 copy-start.2
  0.7 0.0 copy-start.3
  0.7 0.0 copy-start.4
  0.7 0.0 copy-start.5
  0.7 0.0 copy-start.6
  0.7 0.0 copy-start.7
  0.7 0.8 %copy-done = f32[27,2,8,128]{3,2,1,0:T(8,128)S(1)} copy-done((f32[27,2,8,128]{3,2,1,0:T(8,128)S(1)}, f32[27,2,8,128]{3,2,1,0:T(8,128)}, u32[]{:S(2)}) %copy-start) | copy-done | bytes 221208
  1.6 0.0 copy-done.1
  1.6 0.0 copy-done.2
  1.6 0.0 copy-done.3
  1.6 0.0 copy-done.4
  1.6 0.0 copy-done.5
  1.6 0.0 copy-done.6
  1.6 0.0 copy-done.7
  1.6 9.5 %lattice_step.1 = f32[27,2,8,128]{3,2,1,0:T(8,128)S(1)} custom-call(f32[8,128]{1,0:T(8,128)S(1)} %pause.1.gate, f32[27,2,8,128]{3,2,1,0:T(8,128)S(1)} %copy-done, f32[1,27]{1,0:T(1,128)S(1)} %bitcast.1, s32[2,8,128]{2,1,0:T(8,128)S(1)} %copy-done.1, s32[1,1,256]{2,1,0:T(1,128)S(1)} %copy-done.4, s32[1,1,256]{2,1,0:T(1,128)S(1)} %copy-done.5, ...), custom_call_target="tpu_custom_call" | custom-call | tf_op jit(solution)/shard_map/lattice_step/pallas_call | solution.py:618
  11.1 0.7 %copy.11 = f32[27,2,8,128]{3,2,1,0:T(8,128)} copy(f32[27,2,8,128]{3,2,1,0:T(8,128)S(1)} %lattice_step.1) | data formatting | bytes 442368
  (1 shorter events, 0.0 us)
Async XLA Ops:
  0.7 0.9 %copy-start = (f32[27,2,8,128]{3,2,1,0:T(8,128)S(1)}, f32[27,2,8,128]{3,2,1,0:T(8,128)}, u32[]{:S(2)}) copy-start(f32[27,2,8,128]{3,2,1,0:T(8,128)} %pop.1) | copy-start | bytes 663556
  0.7 0.9 %copy-start.1 = (s32[2,8,128]{2,1,0:T(8,128)S(1)}, s32[2,8,128]{2,1,0:T(8,128)}, u32[]{:S(2)}) copy-start(s32[2,8,128]{2,1,0:T(8,128)} %solid.1) | copy-start | bytes 24580
  0.7 0.9 %copy-start.2 = (s32[1,1,8,256]{3,2,1,0:T(8,128)S(1)}, s32[1,1,8,256]{3,2,1,0:T(8,128)}, u32[]{:S(2)}) copy-start(s32[1,1,8,256]{3,2,1,0:T(8,128)} %stencil.1) | copy-start | bytes 24580
  0.7 0.9 %copy-start.3 = (f32[1,1,8,256]{3,2,1,0:T(8,128)S(1)}, f32[1,1,8,256]{3,2,1,0:T(8,128)}, u32[]{:S(2)}) copy-start(f32[1,1,8,256]{3,2,1,0:T(8,128)} %weight.1) | copy-start | bytes 24580
  0.7 0.9 %copy-start.4 = (s32[1,1,256]{2,1,0:T(1,128)S(1)}, s32[1,1,256]{2,1,0:T(1,128)}, u32[]{:S(2)}) copy-start(s32[1,1,256]{2,1,0:T(1,128)} %wall.1) | copy-start | bytes 3076
  0.7 0.9 %copy-start.5 = (s32[1,1,256]{2,1,0:T(1,128)S(1)}, s32[1,1,256]{2,1,0:T(1,128)}, u32[]{:S(2)}) copy-start(s32[1,1,256]{2,1,0:T(1,128)} %normal.1) | copy-start | bytes 3076
  0.7 0.9 %copy-start.6 = (s32[1,1,256]{2,1,0:T(1,128)S(1)}, s32[1,1,256]{2,1,0:T(1,128)}, u32[]{:S(2)}) copy-start(s32[1,1,256]{2,1,0:T(1,128)} %ref.1) | copy-start | bytes 3076
  0.7 0.9 %copy-start.7 = (f32[27]{0:T(128)S(1)}, f32[27]{0:T(128)}, u32[]{:S(2)}) copy-start(f32[27]{0:T(128)} %param.10) | copy-start | bytes 328

commit v5 on v4

--- a/solution.py
+++ b/solution.py
@@ -97,6 +97,130 @@
     )
 
 
+def equilibrium_terms(n):
+    square = [value * value for value in n]
+    return 1.0 - 1.5 * (square[0] + square[1] + square[2])
+
+
+def along(n, step):
+    total = None
+    for c in range(3):
+        if step[c] > 0:
+            total = plus(total, n[c])
+        elif step[c] < 0:
+            total = minus(total, n[c])
+    return total
+
+
+def decode(code, slots, offset):
+    r = code.astype(jnp.int32) - 1
+    owner = jnp.right_shift(r, slots.bit_length() - 1)
+    return owner, jnp.bitwise_and(r, slots - 1) + offset
+
+
+def lookup(devices_y, owner, lane, axis, operand):
+    value = [jnp.zeros(lane.shape, jnp.float32)] * 3
+    for peer in range(devices_y):
+        here = owner == peer
+        for c in range(3):
+            value[c] = jnp.where(
+                here,
+                jnp.take_along_axis(operand(peer, c), lane, axis=1, mode="promise_in_bounds"),
+                value[c],
+            )
+    ratio = np.float32(wall_ratio)
+    return [jnp.where(axis == np.float32(c), 0.0, value[c] * ratio) for c in range(3)]
+
+
+def wrap(value, size):
+    return jnp.where(value < 0, value + size, jnp.where(value >= size, value - size, value))
+
+
+def part_of(owner, slots):
+    return (owner * slots) // LANES * 3, lax.rem(owner * slots, LANES)
+
+
+def mend(value, line, b):
+    size_y = value.shape[0]
+    row_line = lax.broadcasted_iota(jnp.int32, value.shape, 0)
+    edge = 0 if b > 0 else size_y - 1
+    return jnp.where(row_line == edge, jnp.broadcast_to(line, value.shape), value)
+
+
+def far_side(way, devices_y, slots_all, moved, got_face, got_corner, rx_x, settled, x):
+    a = 1 - 2 * way
+    tile = got_face.shape[2:]
+    slots = slots_all // devices_y
+    my_y = lax.axis_index("gy")
+    part, offset = part_of(my_y, slots)
+    part0, offset0 = part_of(wrap(my_y - 1, devices_y), slots)
+    part1, offset1 = part_of(wrap(my_y + 1, devices_y), slots)
+    upper = lax.broadcasted_iota(jnp.int32, tile, 0) == 0
+
+    def spread(line):
+        return jnp.broadcast_to(line, tile)
+
+    def stack(one, other):
+        return jnp.where(upper, spread(one), spread(other))
+
+    quantity = [
+        stack(got_corner[way, 0, f : f + 1, :], got_corner[way, 1, f : f + 1, :]) for f in range(7)
+    ]
+    n = lookup(
+        devices_y,
+        *decode(quantity[4], slots, jnp.where(upper, offset0, offset1)),
+        quantity[5],
+        lambda peer, c: stack(
+            rx_x[way, peer, pl.ds(part0 + c, 1), :], rx_x[way, peer, pl.ds(part1 + c, 1), :]
+        ),
+    )
+    n[1] = jnp.where(upper, n[1], -n[1])
+    rest = equilibrium_terms(n)
+    corners, marked = ([], [])
+    for c in (-1, 0, 1):
+        s = along(n, (a, 1, c))
+        value = quantity[c + 1] + quantity[3] * (rest + s * (3.0 + 4.5 * s))
+        corners.append(roll(value, c, 1))
+        marked.append(roll(quantity[6], c, 1))
+    n = lookup(
+        devices_y,
+        *decode(got_face[way, 10], slots, offset),
+        got_face[way, 11],
+        lambda peer, c: spread(rx_x[way, peer, pl.ds(part + c, 1), :]),
+    )
+    rho = got_face[way, 9]
+    rest = equilibrium_terms(n)
+    tiles = []
+    for k in range(9):
+        b, c = (k // 3 - 1, k % 3 - 1)
+        i = (a + 1) * 9 + k
+        s = along(n, (a, b, c))
+        value = moved[way, k] + roll(roll(rho * (rest + s * (3.0 + 4.5 * s)), b, 0), c, 1)
+        mark = moved[way, 9 + k]
+        if b != 0:
+            q = 0 if b > 0 else 1
+            value = mend(value, corners[c + 1][q : q + 1, :], b)
+            mark = mend(mark, marked[c + 1][q : q + 1, :], b)
+        tiles.append(jnp.where(mark != 0, settled[26 - i, x], value))
+    return tiles
+
+
+def finish(devices_y, slots_all, early, settled, moved, got_face, got_corner, rx_x, out, late, sem):
+    copies = [
+        pltpu.make_async_copy(early.at[0:18], out.at[0:18], sem.at[0]),
+        pltpu.make_async_copy(early.at[18:27, 1:], out.at[18:27, 1:], sem.at[1]),
+        pltpu.make_async_copy(late, out.at[18:27, 0], sem.at[2]),
+    ]
+    copies[0].start()
+    copies[1].start()
+    tiles = far_side(0, devices_y, slots_all, moved, got_face, got_corner, rx_x, settled, 0)
+    for k, value in enumerate(tiles):
+        late[k] = value
+    copies[2].start()
+    for copy in copies:
+        copy.wait()
+
+
 def kernel(
     devices_x,
     devices_y,
@@ -111,23 +235,23 @@
     stencil,
     weight,
     out,
+    settled,
+    moved,
+    got_face,
+    got_corner,
+    rx_x,
     vel,
     samples,
     rx_row,
-    rx_x,
     post,
-    settled,
     shifted,
     fields,
     face,
     near,
     corner,
-    got_face,
     got_near,
-    got_corner,
     lines,
     masks,
-    moved,
     tally,
     send_sem,
     near_sem,
@@ -144,11 +268,7 @@
     shift_bits = slots.bit_length() - 1
     my_x = lax.axis_index("gx")
     my_y = lax.axis_index("gy")
-    ratio = np.float32(wall_ratio)
     tile = (size_y, LANES)
-
-    def wrap(value, size):
-        return jnp.where(value < 0, value + size, jnp.where(value >= size, value - size, value))
 
     barrier = pltpu.get_barrier_semaphore()
     columns = {dy: wrap(my_y + dy, devices_y) for dy in range(devices_y)}
@@ -236,19 +356,6 @@
             n = part * 3 + c
             samples[n : n + 1, :] = jnp.sum(picked[c] * factor, axis=0, keepdims=True)
     rx_row[my_y] = samples[...]
-
-    def equilibrium_terms(n):
-        square = [value * value for value in n]
-        return 1.0 - 1.5 * (square[0] + square[1] + square[2])
-
-    def along(n, step):
-        total = None
-        for c in range(3):
-            if step[c] > 0:
-                total = plus(total, n[c])
-            elif step[c] < 0:
-                total = minus(total, n[c])
-        return total
 
     def pairs(rho, n):
         rest = rho * equilibrium_terms(n)
@@ -414,33 +521,10 @@
         expect(ready.at[3], devices_y - below)
         send_where(0, beyond)
 
-    def decode(code, offset):
-        r = code.astype(jnp.int32) - 1
-        return jnp.right_shift(r, shift_bits), jnp.bitwise_and(r, slots - 1) + offset
-
-    def lookup(owner, lane, axis, operand):
-        value = [jnp.zeros(tile, jnp.float32)] * 3
-        for peer in range(devices_y):
-            here = owner == peer
-            for c in range(3):
-                value[c] = jnp.where(
-                    here,
-                    jnp.take_along_axis(operand(peer, c), lane, axis=1, mode="promise_in_bounds"),
-                    value[c],
-                )
-        return [jnp.where(axis == np.float32(c), 0.0, value[c] * ratio) for c in range(3)]
-
     def spread(line):
         return jnp.broadcast_to(line, tile)
 
-    def part_of(owner):
-        return (owner * slots) // LANES * 3, lax.rem(owner * slots, LANES)
-
-    def mend(value, line, b):
-        edge = 0 if b > 0 else size_y - 1
-        return jnp.where(row_line == edge, spread(line), value)
-
-    part, offset = part_of(my_y)
+    part, offset = part_of(my_y, slots)
 
     near_total = 2 * near.shape[1] + (devices_y - 1) * used
     near_count = pltpu.make_async_copy(
@@ -451,7 +535,8 @@
     near_count.wait()
     for x in range(size_x):
         n = lookup(
-            *decode(fields[1, x], offset),
+            devices_y,
+            *decode(fields[1, x], slots, offset),
             fields[2, x],
             lambda peer, c: spread(rx_row[peer, pl.ds(part + c, 1), :]),
         )
@@ -472,10 +557,11 @@
                 q = side * size_x + x
                 lines[9 + f, q : q + 1, :] = got_near[side, n : n + 1, :]
     lower = row_line < size_x
-    part0, offset0 = part_of(columns[-1])
-    part1, offset1 = part_of(columns[1])
+    part0, offset0 = part_of(columns[-1], slots)
+    part1, offset1 = part_of(columns[1], slots)
     n = lookup(
-        *decode(lines[10], jnp.where(lower, offset0, offset1)),
+        devices_y,
+        *decode(lines[10], slots, jnp.where(lower, offset0, offset1)),
         lines[11],
         lambda peer, c: jnp.where(
             lower,
@@ -522,12 +608,6 @@
         expect(ready.at[1], devices_y - below)
         send_where(1, beyond)
 
-    upper = row_line == 0
-    sideways = jnp.where(upper, offset0, offset1)
-
-    def stack(one, other):
-        return jnp.where(upper, spread(one), spread(other))
-
     far_total = devices_y * used + 2 * corner.shape[2]
     for way, a in ((1, -1), (0, 1)):
         pltpu.make_async_copy(got_face.at[way], got_face.at[way], face_sem.at[way]).wait()
@@ -535,48 +615,16 @@
             b, c = (k // 3 - 1, k % 3 - 1)
             moved[way, k] = roll(roll(got_face[way, k], b, 0), c, 1)
             moved[way, 9 + k] = roll(roll(got_face[way, 12], b, 0), c, 1)
-        found_at = decode(got_face[way, 10], offset)
         pltpu.make_async_copy(
             tally.at[0:far_total], tally.at[0:far_total], far_sem.at[way]
         ).wait()
-        quantity = [
-            stack(got_corner[way, 0, f : f + 1, :], got_corner[way, 1, f : f + 1, :])
-            for f in range(7)
-        ]
-        n = lookup(
-            *decode(quantity[4], sideways),
-            quantity[5],
-            lambda peer, c: stack(
-                rx_x[way, peer, pl.ds(part0 + c, 1), :], rx_x[way, peer, pl.ds(part1 + c, 1), :]
-            ),
-        )
-        n[1] = jnp.where(upper, n[1], -n[1])
-        rest = equilibrium_terms(n)
-        corners, marked = ([], [])
-        for c in (-1, 0, 1):
-            s = along(n, (a, 1, c))
-            value = quantity[c + 1] + quantity[3] * (rest + s * (3.0 + 4.5 * s))
-            corners.append(roll(value, c, 1))
-            marked.append(roll(quantity[6], c, 1))
-        n = lookup(
-            *found_at,
-            got_face[way, 11],
-            lambda peer, c: spread(rx_x[way, peer, pl.ds(part + c, 1), :]),
-        )
-        rho = got_face[way, 9]
-        rest = equilibrium_terms(n)
-        x = 0 if a > 0 else size_x - 1
-        for k in range(9):
-            b, c = (k // 3 - 1, k % 3 - 1)
-            i = (a + 1) * 9 + k
-            s = along(n, (a, b, c))
-            value = moved[way, k] + roll(roll(rho * (rest + s * (3.0 + 4.5 * s)), b, 0), c, 1)
-            mark = moved[way, 9 + k]
-            if b != 0:
-                q = 0 if b > 0 else 1
-                value = mend(value, corners[c + 1][q : q + 1, :], b)
-                mark = mend(mark, marked[c + 1][q : q + 1, :], b)
-            out[i, x] = jnp.where(mark != 0, settled[26 - i, x], value)
+        if way == 1:
+            x = size_x - 1
+            tiles = far_side(
+                way, devices_y, slots_all, moved, got_face, got_corner, rx_x, settled, x
+            )
+            for k, value in enumerate(tiles):
+                out[k, x] = value
     pltpu.make_async_copy(tally, tally, send_sem).wait()
 
 
@@ -615,29 +663,32 @@
         cost_estimate=pl.CostEstimate(flops=10**9, bytes_accessed=4096, transcendentals=0),
         name="pause",
     )()
-    result = pl.pallas_call(
+    kept = [
+        populations.shape,
+        populations.shape,
+        (2, 18) + tile,
+        (2, 13) + tile,
+        (2, 2, 8, LANES),
+        (2, devices_y, held, LANES),
+    ]
+    results = pl.pallas_call(
         functools.partial(kernel, devices_x, devices_y),
-        out_shape=pltpu.VMEM(populations.shape, f32),
+        out_shape=[pltpu.VMEM(shape, f32) for shape in kept],
         in_specs=[on_core] * 6 + [scalars] + [on_core] * 3,
-        out_specs=pl.BlockSpec(memory_space=pltpu.VMEM),
+        out_specs=[on_core] * len(kept),
         scratch_shapes=[
             vmem((3 * size_x * size_y, LANES), f32),
             vmem((held, LANES), f32),
             vmem((devices_y, held, LANES), f32),
-            vmem((2, devices_y, held, LANES), f32),
-            vmem(populations.shape, f32),
             vmem(populations.shape, f32),
             vmem(populations.shape, f32),
             vmem((3, size_x) + tile, f32),
             vmem((2, 13) + tile, f32),
             vmem((2, near_lines, LANES), f32),
             vmem((2, 2, 8, LANES), f32),
-            vmem((2, 13) + tile, f32),
             vmem((2, near_lines, LANES), f32),
-            vmem((2, 2, 8, LANES), f32),
             vmem((13,) + tile, f32),
             vmem((9, size_x) + tile, f32),
-            vmem((2, 18) + tile, f32),
             vmem((sent, LANES), f32),
             dma,
             dma,
@@ -661,7 +712,14 @@
         near_core(cells),
         near_core(factors),
     )
-    return pltpu.with_memory_space_constraint(result, pltpu.VMEM)
+    return pl.pallas_call(
+        functools.partial(finish, devices_y, slots_all),
+        out_shape=jax.ShapeDtypeStruct(populations.shape, f32),
+        in_specs=[on_core] * len(kept),
+        out_specs=pl.BlockSpec(memory_space=pl.ANY),
+        scratch_shapes=[vmem((9,) + tile, f32), dma((3,))],
+        name="finish",
+    )(*[near_core(value) for value in results])
 
 
 def solution(mesh):

time: 11.9 us -> 11.9 us (level)
  local copies, waits for them, and re-layouts: 1.57 us -> 0.88 us
  Pallas kernels: 9.46 us -> 10.1 us
    pallas_call x0 -> x1, Pallas kernels: none -> 0.84 us  [local(): pl.pallas_call(functools.partial(finish, devices_y, slots_all), out_shape...]
    unnamed x17 -> x16, local copies, waits for them, and re-layouts: 1.57 us -> 0.88 us
    pallas_call x1, Pallas kernels: 9.46 us -> 9.28 us  [local(): pl.pallas_call(functools.partial(kernel, devices_x, devices_y), out_shape...]
where the time goes in v5:
time: 11.9 us; the launch traced here: 11.8 us
  Pallas kernels  10.1 us (85%)
  local copies, waits for them, and re-layouts  0.88 us (7%)
  between operations  0.76 us (6%)
    pallas_call x1, Pallas kernels, local(): pl.pallas_call(functools.partial(kernel, devices_x, devices_y), out_shape...  9.28 us
    unnamed x16, local copies, waits for them, and re-layouts  0.88 us
    pallas_call x1, Pallas kernels, local(): pl.pallas_call(functools.partial(finish, devices_y, slots_all), out_shape...  0.84 us

profile of v5, /device:TPU:0, one launch (start us, length us, event | category | flops | bytes accessed | tf_op | source)
XLA Modules:
  0.0 11.8 jit_solution(11711879581128455809)
XLA Ops:
  0.7 0.0 copy-start
  0.7 0.0 copy-start.1
  0.7 0.0 copy-start.2
  0.7 0.0 copy-start.3
  0.7 0.0 copy-start.4
  0.7 0.0 copy-start.5
  0.7 0.0 copy-start.6
  0.7 0.0 copy-start.7
  0.7 0.8 %copy-done = f32[27,2,8,128]{3,2,1,0:T(8,128)S(1)} copy-done((f32[27,2,8,128]{3,2,1,0:T(8,128)S(1)}, f32[27,2,8,128]{3,2,1,0:T(8,128)}, u32[]{:S(2)}) %copy-start) | copy-done | bytes 221208
  1.6 0.0 copy-done.1
  1.6 0.0 copy-done.2
  1.6 0.0 copy-done.3
  1.6 0.0 copy-done.4
  1.6 0.0 copy-done.5
  1.6 0.0 copy-done.6
  1.6 0.0 copy-done.7
  1.6 9.3 %lattice_step.1 = (f32[27,2,8,128]{3,2,1,0:T(8,128)S(1)}, f32[27,2,8,128]{3,2,1,0:T(8,128)S(1)}, f32[2,18,8,128]{3,2,1,0:T(8,128)S(1)}, f32[2,13,8,128]{3,2,1,0:...) custom-call(f32[8,128]{1,0:T(8,128)S(1)} %pause.1.gate, f32[27,2,8,128]{3,2,1,0:T(8,128)S(1)} %copy-done, ...), custom_call_target="tpu_custom_call" | custom-call | tf_op jit(solution)/shard_map/lattice_step/pallas_call | solution.py:674
  10.9 0.8 %finish.1 = f32[27,2,8,128]{3,2,1,0:T(8,128)} custom-call(f32[27,2,8,128]{3,2,1,0:T(8,128)S(1)} %get-tuple-element.11.early, f32[27,2,8,128]{3,2,1,0:T(8,128)S(1)} %get-tuple-element.12.settled, f32[2,18,8,128]{3,2,1,0:T(8,128)S(1)} %get-tuple-element.13.moved, f32[2,13,8,128]{3,2,1,0:T(8,128)S(1)} %get-tuple-element.14.got_face, ...), custom_call_target="tpu_custom_call" | custom-call | tf_op jit(solution)/shard_map/finish/pallas_call | solution.py:715
  (1 shorter events, 0.0 us)
Async XLA Ops:
  0.7 0.9 %copy-start = (f32[27,2,8,128]{3,2,1,0:T(8,128)S(1)}, f32[27,2,8,128]{3,2,1,0:T(8,128)}, u32[]{:S(2)}) copy-start(f32[27,2,8,128]{3,2,1,0:T(8,128)} %pop.1) | copy-start | bytes 663556
  0.7 0.9 %copy-start.1 = (s32[2,8,128]{2,1,0:T(8,128)S(1)}, s32[2,8,128]{2,1,0:T(8,128)}, u32[]{:S(2)}) copy-start(s32[2,8,128]{2,1,0:T(8,128)} %solid.1) | copy-start | bytes 24580
  0.7 0.9 %copy-start.2 = (s32[1,1,8,256]{3,2,1,0:T(8,128)S(1)}, s32[1,1,8,256]{3,2,1,0:T(8,128)}, u32[]{:S(2)}) copy-start(s32[1,1,8,256]{3,2,1,0:T(8,128)} %stencil.1) | copy-start | bytes 24580
  0.7 0.9 %copy-start.3 = (f32[1,1,8,256]{3,2,1,0:T(8,128)S(1)}, f32[1,1,8,256]{3,2,1,0:T(8,128)}, u32[]{:S(2)}) copy-start(f32[1,1,8,256]{3,2,1,0:T(8,128)} %weight.1) | copy-start | bytes 24580
  0.7 0.9 %copy-start.4 = (s32[1,1,256]{2,1,0:T(1,128)S(1)}, s32[1,1,256]{2,1,0:T(1,128)}, u32[]{:S(2)}) copy-start(s32[1,1,256]{2,1,0:T(1,128)} %wall.1) | copy-start | bytes 3076
  0.7 0.9 %copy-start.5 = (s32[1,1,256]{2,1,0:T(1,128)S(1)}, s32[1,1,256]{2,1,0:T(1,128)}, u32[]{:S(2)}) copy-start(s32[1,1,256]{2,1,0:T(1,128)} %normal.1) | copy-start | bytes 3076
  0.7 0.9 %copy-start.6 = (s32[1,1,256]{2,1,0:T(1,128)S(1)}, s32[1,1,256]{2,1,0:T(1,128)}, u32[]{:S(2)}) copy-start(s32[1,1,256]{2,1,0:T(1,128)} %ref.1) | copy-start | bytes 3076
  0.7 0.9 %copy-start.7 = (f32[27]{0:T(128)S(1)}, f32[27]{0:T(128)}, u32[]{:S(2)}) copy-start(f32[27]{0:T(128)} %param.10) | copy-start | bytes 328

commit v6 on v5

--- a/solution.py
+++ b/solution.py
@@ -295,7 +295,16 @@
     outward = jnp.where(at_last, devices_y, inner)
     across = sorted(range(devices_y), key=lambda dy: -min(dy, devices_y - dy))
     for dy in across:
-        when(columns[dy] >= inward, barrier, -1, dy)
+
+        @pl.when(columns[dy] >= inward)
+        def _(dy=dy):
+            pl.semaphore_signal(
+                barrier,
+                inc=1,
+                device_id={"gx": last, "gy": columns[dy]},
+                device_id_type=MESH,
+            )
+
     for dy in across:
         when(columns[dy] >= outward, barrier, 1, dy)
     for dy in range(1, devices_y):
@@ -452,7 +461,8 @@
             if dy == corner_dy:
                 send(corner.at[way, side], got_corner.at[way, side], far_sem.at[way], dx, dy)
         if dy == 0:
-            send(face.at[way], got_face.at[way], face_sem.at[way], dx, dy)
+            sem = far_sem.at[1] if way else face_sem
+            send(face.at[way], got_face.at[way], sem, dx, dy)
 
     def expect(sem, amount):
         pl.when(amount > 0)(lambda: pl.semaphore_wait(sem, amount))
@@ -610,15 +620,19 @@
 
     far_total = devices_y * used + 2 * corner.shape[2]
     for way, a in ((1, -1), (0, 1)):
-        pltpu.make_async_copy(got_face.at[way], got_face.at[way], face_sem.at[way]).wait()
+        total = far_total
+        if way == 0:
+            pltpu.make_async_copy(got_face.at[way], got_face.at[way], face_sem).wait()
+        else:
+            total += got_face.shape[1] * size_y
+            pltpu.make_async_copy(tally.at[0:total], tally.at[0:total], far_sem.at[way]).wait()
         for k in range(9):
             b, c = (k // 3 - 1, k % 3 - 1)
             moved[way, k] = roll(roll(got_face[way, k], b, 0), c, 1)
             moved[way, 9 + k] = roll(roll(got_face[way, 12], b, 0), c, 1)
-        pltpu.make_async_copy(
-            tally.at[0:far_total], tally.at[0:far_total], far_sem.at[way]
-        ).wait()
-        if way == 1:
+        if way == 0:
+            pltpu.make_async_copy(tally.at[0:total], tally.at[0:total], far_sem.at[way]).wait()
+        else:
             x = size_x - 1
             tiles = far_side(
                 way, devices_y, slots_all, moved, got_face, got_corner, rx_x, settled, x
@@ -692,7 +706,7 @@
             vmem((sent, LANES), f32),
             dma,
             dma,
-            dma((2,)),
+            dma,
             dma((2,)),
             regular,
             regular,

time: 11.9 us -> 11.9 us (level)
  no operation moved by 1% of the time
where the time goes in v6:
time: 11.9 us; the launch traced here: 11.8 us
  Pallas kernels  10.1 us (85%)
  local copies, waits for them, and re-layouts  0.88 us (7%)
  between operations  0.76 us (6%)
    pallas_call x1, Pallas kernels, local(): pl.pallas_call(functools.partial(kernel, devices_x, devices_y), out_shape...  9.27 us
    unnamed x16, local copies, waits for them, and re-layouts  0.88 us
    pallas_call x1, Pallas kernels, local(): pl.pallas_call(functools.partial(finish, devices_y, slots_all), out_shape...  0.84 us

profile of v6, /device:TPU:0, one launch (start us, length us, event | category | flops | bytes accessed | tf_op | source)
XLA Modules:
  0.0 11.8 jit_solution(4152258605748130296)
XLA Ops:
  0.7 0.0 copy-start
  0.7 0.0 copy-start.1
  0.7 0.0 copy-start.2
  0.7 0.0 copy-start.3
  0.7 0.0 copy-start.4
  0.7 0.0 copy-start.5
  0.7 0.0 copy-start.6
  0.7 0.0 copy-start.7
  0.7 0.8 %copy-done = f32[27,2,8,128]{3,2,1,0:T(8,128)S(1)} copy-done((f32[27,2,8,128]{3,2,1,0:T(8,128)S(1)}, f32[27,2,8,128]{3,2,1,0:T(8,128)}, u32[]{:S(2)}) %copy-start) | copy-done | bytes 221208
  1.6 0.0 copy-done.1
  1.6 0.0 copy-done.2
  1.6 0.0 copy-done.3
  1.6 0.0 copy-done.4
  1.6 0.0 copy-done.5
  1.6 0.0 copy-done.6
  1.6 0.0 copy-done.7
  1.6 9.3 %lattice_step.1 = (f32[27,2,8,128]{3,2,1,0:T(8,128)S(1)}, f32[27,2,8,128]{3,2,1,0:T(8,128)S(1)}, f32[2,18,8,128]{3,2,1,0:T(8,128)S(1)}, f32[2,13,8,128]{3,2,1,0:...) custom-call(f32[8,128]{1,0:T(8,128)S(1)} %pause.1.gate, f32[27,2,8,128]{3,2,1,0:T(8,128)S(1)} %copy-done, ...), custom_call_target="tpu_custom_call" | custom-call | tf_op jit(solution)/shard_map/lattice_step/pallas_call | solution.py:688
  10.9 0.8 %finish.1 = f32[27,2,8,128]{3,2,1,0:T(8,128)} custom-call(f32[27,2,8,128]{3,2,1,0:T(8,128)S(1)} %get-tuple-element.11.early, f32[27,2,8,128]{3,2,1,0:T(8,128)S(1)} %get-tuple-element.12.settled, f32[2,18,8,128]{3,2,1,0:T(8,128)S(1)} %get-tuple-element.13.moved, f32[2,13,8,128]{3,2,1,0:T(8,128)S(1)} %get-tuple-element.14.got_face, ...), custom_call_target="tpu_custom_call" | custom-call | tf_op jit(solution)/shard_map/finish/pallas_call | solution.py:729
  (1 shorter events, 0.0 us)
Async XLA Ops:
  0.7 0.9 %copy-start = (f32[27,2,8,128]{3,2,1,0:T(8,128)S(1)}, f32[27,2,8,128]{3,2,1,0:T(8,128)}, u32[]{:S(2)}) copy-start(f32[27,2,8,128]{3,2,1,0:T(8,128)} %pop.1) | copy-start | bytes 663556
  0.7 0.9 %copy-start.1 = (s32[2,8,128]{2,1,0:T(8,128)S(1)}, s32[2,8,128]{2,1,0:T(8,128)}, u32[]{:S(2)}) copy-start(s32[2,8,128]{2,1,0:T(8,128)} %solid.1) | copy-start | bytes 24580
  0.7 0.9 %copy-start.2 = (s32[1,1,8,256]{3,2,1,0:T(8,128)S(1)}, s32[1,1,8,256]{3,2,1,0:T(8,128)}, u32[]{:S(2)}) copy-start(s32[1,1,8,256]{3,2,1,0:T(8,128)} %stencil.1) | copy-start | bytes 24580
  0.7 0.9 %copy-start.3 = (f32[1,1,8,256]{3,2,1,0:T(8,128)S(1)}, f32[1,1,8,256]{3,2,1,0:T(8,128)}, u32[]{:S(2)}) copy-start(f32[1,1,8,256]{3,2,1,0:T(8,128)} %weight.1) | copy-start | bytes 24580
  0.7 0.9 %copy-start.4 = (s32[1,1,256]{2,1,0:T(1,128)S(1)}, s32[1,1,256]{2,1,0:T(1,128)}, u32[]{:S(2)}) copy-start(s32[1,1,256]{2,1,0:T(1,128)} %wall.1) | copy-start | bytes 3076
  0.7 0.9 %copy-start.5 = (s32[1,1,256]{2,1,0:T(1,128)S(1)}, s32[1,1,256]{2,1,0:T(1,128)}, u32[]{:S(2)}) copy-start(s32[1,1,256]{2,1,0:T(1,128)} %normal.1) | copy-start | bytes 3076
  0.7 0.9 %copy-start.6 = (s32[1,1,256]{2,1,0:T(1,128)S(1)}, s32[1,1,256]{2,1,0:T(1,128)}, u32[]{:S(2)}) copy-start(s32[1,1,256]{2,1,0:T(1,128)} %ref.1) | copy-start | bytes 3076
  0.7 0.9 %copy-start.7 = (f32[27]{0:T(128)S(1)}, f32[27]{0:T(128)}, u32[]{:S(2)}) copy-start(f32[27]{0:T(128)} %param.10) | copy-start | bytes 328

commit v7 on v6

--- a/solution.py
+++ b/solution.py
@@ -258,7 +258,6 @@
     face_sem,
     far_sem,
     row_ready,
-    cross,
     ready,
 ):
     size_x, size_y = pop.shape[1:3]
@@ -485,7 +484,8 @@
     beyond = {dy: columns[dy] >= outer for dy in across}
     beneath = {dy: both(columns[dy] >= inner, columns[dy] < outer) for dy in across}
     top = devices_y - 2
-    low = my_y < top
+    low = both(my_y < top, my_x > 0)
+    high = both(my_y >= top, my_x > 0)
     ahead = [(at_last, 1, 0, 0), (my_x > 0, -1, 1, 2)]
     expect(
         barrier,
@@ -504,17 +504,17 @@
                 send_where(way, inside)
 
     for dy in range(1, devices_y):
-        crossing = both(jnp.logical_not(low), columns[dy] < top) if dy % 2 == 0 else None
+        crossing = both(high, columns[dy] < top) if dy % 2 == 0 else None
         lower = my_y + dy >= devices_y
         if crossing is None:
             when(lower, row_ready, 0, dy)
         else:
-            when(crossing, cross, 0, dy)
+            when(crossing, ready.at[0], 0, dy)
             when(both(lower, jnp.logical_not(crossing)), row_ready, 0, dy)
 
     @pl.when(low)
     def _():
-        pl.semaphore_wait(cross, 1)
+        pl.semaphore_wait(ready.at[0], 1)
         for applies, dx, way, n in ahead:
 
             @pl.when(applies)
@@ -709,7 +709,6 @@
             dma,
             dma((2,)),
             regular,
-            regular,
             regular((4,)),
         ],
         compiler_params=pltpu.CompilerParams(collective_id=0, has_side_effects=True),

time: 11.9 us -> 11.9 us (level)
  no operation moved by 1% of the time
where the time goes in v7:
time: 11.9 us; the launch traced here: 11.7 us
  Pallas kernels  10.1 us (85%)
  local copies, waits for them, and re-layouts  0.88 us (7%)
  between operations  0.76 us (6%)
    pallas_call x1, Pallas kernels, local(): pl.pallas_call(functools.partial(kernel, devices_x, devices_y), out_shape...  9.26 us
    unnamed x16, local copies, waits for them, and re-layouts  0.88 us
    pallas_call x1, Pallas kernels, local(): pl.pallas_call(functools.partial(finish, devices_y, slots_all), out_shape...  0.84 us

profile of v7, /device:TPU:0, one launch (start us, length us, event | category | flops | bytes accessed | tf_op | source)
XLA Modules:
  0.0 11.7 jit_solution(1301283789299878624)
XLA Ops:
  0.7 0.0 copy-start
  0.7 0.0 copy-start.1
  0.7 0.0 copy-start.2
  0.7 0.0 copy-start.3
  0.7 0.0 copy-start.4
  0.7 0.0 copy-start.5
  0.7 0.0 copy-start.6
  0.7 0.0 copy-start.7
  0.7 0.8 %copy-done = f32[27,2,8,128]{3,2,1,0:T(8,128)S(1)} copy-done((f32[27,2,8,128]{3,2,1,0:T(8,128)S(1)}, f32[27,2,8,128]{3,2,1,0:T(8,128)}, u32[]{:S(2)}) %copy-start) | copy-done | bytes 221208
  1.6 0.0 copy-done.1
  1.6 0.0 copy-done.2
  1.6 0.0 copy-done.3
  1.6 0.0 copy-done.4
  1.6 0.0 copy-done.5
  1.6 0.0 copy-done.6
  1.6 0.0 copy-done.7
  1.6 9.3 %lattice_step.1 = (f32[27,2,8,128]{3,2,1,0:T(8,128)S(1)}, f32[27,2,8,128]{3,2,1,0:T(8,128)S(1)}, f32[2,18,8,128]{3,2,1,0:T(8,128)S(1)}, f32[2,13,8,128]{3,2,1,0:...) custom-call(f32[8,128]{1,0:T(8,128)S(1)} %pause.1.gate, f32[27,2,8,128]{3,2,1,0:T(8,128)S(1)} %copy-done, ...), custom_call_target="tpu_custom_call" | custom-call | tf_op jit(solution)/shard_map/lattice_step/pallas_call | solution.py:688
  10.9 0.8 %finish.1 = f32[27,2,8,128]{3,2,1,0:T(8,128)} custom-call(f32[27,2,8,128]{3,2,1,0:T(8,128)S(1)} %get-tuple-element.11.early, f32[27,2,8,128]{3,2,1,0:T(8,128)S(1)} %get-tuple-element.12.settled, f32[2,18,8,128]{3,2,1,0:T(8,128)S(1)} %get-tuple-element.13.moved, f32[2,13,8,128]{3,2,1,0:T(8,128)S(1)} %get-tuple-element.14.got_face, ...), custom_call_target="tpu_custom_call" | custom-call | tf_op jit(solution)/shard_map/finish/pallas_call | solution.py:728
  (1 shorter events, 0.0 us)
Async XLA Ops:
  0.7 0.9 %copy-start = (f32[27,2,8,128]{3,2,1,0:T(8,128)S(1)}, f32[27,2,8,128]{3,2,1,0:T(8,128)}, u32[]{:S(2)}) copy-start(f32[27,2,8,128]{3,2,1,0:T(8,128)} %pop.1) | copy-start | bytes 663556
  0.7 0.9 %copy-start.1 = (s32[2,8,128]{2,1,0:T(8,128)S(1)}, s32[2,8,128]{2,1,0:T(8,128)}, u32[]{:S(2)}) copy-start(s32[2,8,128]{2,1,0:T(8,128)} %solid.1) | copy-start | bytes 24580
  0.7 0.9 %copy-start.2 = (s32[1,1,8,256]{3,2,1,0:T(8,128)S(1)}, s32[1,1,8,256]{3,2,1,0:T(8,128)}, u32[]{:S(2)}) copy-start(s32[1,1,8,256]{3,2,1,0:T(8,128)} %stencil.1) | copy-start | bytes 24580
  0.7 0.9 %copy-start.3 = (f32[1,1,8,256]{3,2,1,0:T(8,128)S(1)}, f32[1,1,8,256]{3,2,1,0:T(8,128)}, u32[]{:S(2)}) copy-start(f32[1,1,8,256]{3,2,1,0:T(8,128)} %weight.1) | copy-start | bytes 24580
  0.7 0.9 %copy-start.4 = (s32[1,1,256]{2,1,0:T(1,128)S(1)}, s32[1,1,256]{2,1,0:T(1,128)}, u32[]{:S(2)}) copy-start(s32[1,1,256]{2,1,0:T(1,128)} %wall.1) | copy-start | bytes 3076
  0.7 0.9 %copy-start.5 = (s32[1,1,256]{2,1,0:T(1,128)S(1)}, s32[1,1,256]{2,1,0:T(1,128)}, u32[]{:S(2)}) copy-start(s32[1,1,256]{2,1,0:T(1,128)} %normal.1) | copy-start | bytes 3076
  0.7 0.9 %copy-start.6 = (s32[1,1,256]{2,1,0:T(1,128)S(1)}, s32[1,1,256]{2,1,0:T(1,128)}, u32[]{:S(2)}) copy-start(s32[1,1,256]{2,1,0:T(1,128)} %ref.1) | copy-start | bytes 3076
  0.7 0.9 %copy-start.7 = (f32[27]{0:T(128)S(1)}, f32[27]{0:T(128)}, u32[]{:S(2)}) copy-start(f32[27]{0:T(128)} %param.10) | copy-start | bytes 328
